TPU v7x, 128 devices: a whole 4x4x4 slice. The times are simulated.
128 devices in a mesh: tm: 8 (over x, core), space: 16 (over z, y).
Axes of the slice: x: 4, y: 4, z: 4, core: 2. Of those that a mesh axis runs over, the one named last changes fastest.
Arguments:
- speed: float32 [32, 16, 128], P('space'), may hold values from 0.5 to 1.5
- forcing: float32 [32, 32, 16, 128], P('tm', 'space'), may hold values from -1.8 to 1.8
- guess: float32 [8, 4, 32, 16, 128], P('tm', None, 'space'), may hold values from -8 to 8
- basis: float32 [8, 64, 4, 32, 16, 128], P('tm', None, None, 'space'), may hold values from -1 to 1, as said below
Outputs:
- states: float32 [32, 4, 32, 16, 128], P('tm', None, 'space')
- coords: float32 [8, 64], P('tm')
Inputs may be any that keep to these rules, and one draw needn't show every extreme that they name: The columns of each basis[k] are linearly independent.
All inputs are finite; a program needn't handle non-finite values.
Results may differ from a plain program's by a relative error of at most 0.00018.
Values sent between devices are 32-bit elements; how exact they have to be, the bound alone decides.
A program may use at most 128 MiB of HBM per device.

v0:
```python
import jax
import jax.numpy as jnp
from jax import lax
from jax.sharding import PartitionSpec as P

DT = 0.045
exact_mode = lax.Precision.HIGHEST


def from_behind(value, axis, by):
    size = lax.axis_size(axis)
    pairs = [(i, i + by) for i in range(size) if 0 <= i + by < size]
    return lax.ppermute(value, axis, pairs)


def from_behind_2(value, axis, steps):
    count = lax.axis_size(axis)
    pairs = [(source, (source + steps) % count) for source in range(count)]
    return lax.ppermute(value, axis, pairs)


def sent_to_all(value, axis):
    size = lax.axis_size(axis)
    return lax.all_to_all(
        jnp.broadcast_to(value[None], (size, *value.shape)), axis, 0, 0, tiled=True
    )


def taken_together(value, axis):
    everything = sent_to_all(value, axis)
    return jnp.sum(everything, axis=0)


def shifted_ahead(values, axis):
    size = values.shape[axis]
    rest = lax.slice_in_dim(values, 1, size, axis=axis)
    border = jnp.zeros_like(lax.slice_in_dim(values, 0, 1, axis=axis))
    return jnp.concatenate([rest, border], axis=axis)


def shifted_behind(values, axis):
    size = values.shape[axis]
    rest = lax.slice_in_dim(values, 0, size - 1, axis=axis)
    border = jnp.zeros_like(lax.slice_in_dim(values, 0, 1, axis=axis))
    return jnp.concatenate([border, rest], axis=axis)


def update_flow(state, upper_plane, delta_time):
    pressure = state[..., 0, :, :, :]
    depth = pressure.ndim
    above = jnp.concatenate([pressure[..., 1:, :, :], upper_plane], axis=depth - 3)
    flow_x = state[..., 1, :, :, :] - delta_time * (shifted_ahead(pressure, depth - 2) - pressure)
    flow_y = state[..., 2, :, :, :] - delta_time * (shifted_ahead(pressure, depth - 1) - pressure)
    flow_z = state[..., 3, :, :, :] - delta_time * (above - pressure)
    return (pressure, flow_x, flow_y, flow_z)


def update_pressure(pressure, flow_x, flow_y, flow_z, lower_plane, speed_sq, delta_time):
    depth = pressure.ndim
    below = jnp.concatenate([lower_plane, flow_z[..., :-1, :, :]], axis=depth - 3)
    diverge = (
        flow_x
        - shifted_behind(flow_x, depth - 2)
        + (flow_y - shifted_behind(flow_y, depth - 1))
        + (flow_z - below)
    )
    fresh = pressure - delta_time * speed_sq * diverge
    return jnp.stack([fresh, flow_x, flow_y, flow_z], axis=depth - 3)


def advance_field(state, speed_sq, delta_time, bottom_index):
    upper = from_behind(state[0, :1], "space", -1)
    pressure, flow_x, flow_y, flow_z = update_flow(state, upper, delta_time)
    paired = from_behind(jnp.stack([pressure[-1:], state[3, -1:]], axis=0), "space", 1)
    ghost = paired[1] - delta_time * (pressure[:1] - paired[0])
    lower = jnp.where(bottom_index == 0, jnp.zeros_like(ghost), ghost)
    return update_pressure(pressure, flow_x, flow_y, flow_z, lower, speed_sq, delta_time)


def advance_basis(state, speed_sq, delta_time, bottom_index):
    upper = from_behind(state[:, 0, :1], "space", -1)
    pressure, flow_x, flow_y, flow_z = update_flow(state, upper, delta_time)
    paired = from_behind(jnp.stack([pressure[:, -1:], state[:, 3, -1:]], axis=0), "space", 1)
    ghost = paired[1] - delta_time * (pressure[:, :1] - paired[0])
    lower = jnp.where(bottom_index == 0, jnp.zeros_like(ghost), ghost)
    return update_pressure(pressure, flow_x, flow_y, flow_z, lower, speed_sq, delta_time)


def solve_gram(chol, coef):
    lifted = lax.linalg.triangular_solve(chol, coef[..., None], left_side=True, lower=True)
    solved = lax.linalg.triangular_solve(chol, lifted, left_side=True, lower=True, transpose_a=True)
    return solved[..., 0]


def body(speed, forcing, guess, basis):
    bottom_index = lax.axis_index("space")
    speed_sq = speed * speed

    def fine_step(state, row_index):
        moved = advance_field(state, speed_sq, DT, bottom_index)
        return moved.at[0].add(forcing[row_index])

    def sweep(left):
        points = []
        current = left
        for row_index in range(3):
            current = fine_step(current, row_index)
            points.append(current)
        return points

    left = from_behind_2(guess[0], "tm", 1)
    first_points = sweep(left)
    relaxed = fine_step(first_points[-1], 3)
    left = from_behind_2(relaxed, "tm", 1)
    second_points = sweep(left)
    residue = fine_step(second_points[-1], 3) - relaxed
    columns = basis[0]
    moved_columns = columns
    for repeat in range(4):
        moved_columns = advance_basis(moved_columns, speed_sq, DT, bottom_index)
    coarse_columns = advance_basis(columns, speed_sq, 4 * DT, bottom_index)
    corrections = (moved_columns - coarse_columns).reshape(columns.shape[0], -1)
    flat_basis = columns.reshape(columns.shape[0], -1)
    gram = taken_together(jnp.dot(flat_basis, flat_basis.T, precision=exact_mode), "space")
    chol = jnp.linalg.cholesky(gram)

    def candidate(levels):
        left_value = from_behind_2(levels, "tm", 1)
        moved = advance_field(left_value, speed_sq, 4 * DT, bottom_index)
        partial_value = jnp.dot(flat_basis, left_value.reshape(-1), precision=exact_mode)
        coef = taken_together(partial_value, "space")
        weights = solve_gram(chol, coef)
        extra = jnp.dot(weights, corrections, precision=exact_mode).reshape(left_value.shape)
        return moved + extra + residue

    levels = candidate(residue)
    levels = candidate(levels)
    gap = candidate(levels) - levels
    total = gap
    total = (
        advance_field(
            advance_field(from_behind(total, "tm", 4), speed_sq, 8 * DT, bottom_index),
            speed_sq,
            8 * DT,
            bottom_index,
        )
        + gap
    )
    levels = candidate(levels + total)
    final_c = relaxed + levels
    left = from_behind_2(final_c, "tm", 1)
    third_points = sweep(left)
    states = jnp.stack(third_points + [final_c], axis=0)
    partial_value = jnp.dot(flat_basis, final_c.reshape(-1), precision=exact_mode)
    coef = taken_together(partial_value, "space")
    coords = solve_gram(chol, coef)[None, :]
    return (states, coords)


def solution(mesh):
    placed = (
        P("space", None, None),
        P("tm", "space", None, None),
        P("tm", None, "space", None, None),
        P("tm", None, None, "space", None, None),
    )
    return jax.shard_map(
        body,
        mesh=mesh,
        in_specs=placed,
        out_specs=(P("tm", None, "space", None, None), P("tm", None)),
        check_vma=False,
    )
```

profile of v0, /device:TPU:38, one launch (start us, length us, event | category | flops | bytes accessed | tf_op | source)
XLA Modules:
  0.0 460.0 jit_solution(17763336401703002379)
XLA Ops:
  0.7 3.9 collective-permute-done
  4.5 4.5 collective-permute-start.1
  11.1 5.8 %collective-permute-done.2 = f32[2,1,16,128]{3,2,1,0:T(8,128)S(1)} collective-permute-done((f32[2,1,16,128]{3,2,1,0:T(8,128)S(1)}, f32[2,1,16,128]{3,2,1,0:T(8,128)S(1)}, u32[]{:S(2)}, u32[]{:S(2)}) %collective-permute-start.2) | collective-permute-done | bytes 16416 | tf_op jit(solution)/shard_map/ppermute | solution.py:13
  19.7 3.5 collective-permute-done.3
  25.2 5.8 %collective-permute-done.4 = f32[2,1,16,128]{3,2,1,0:T(8,128)S(1)} collective-permute-done((f32[2,1,16,128]{3,2,1,0:T(8,128)S(1)}, f32[2,1,16,128]{3,2,1,0:T(8,128)S(1)}, u32[]{:S(2)}, u32[]{:S(2)}) %collective-permute-start.4) | collective-permute-done | bytes 16416 | tf_op jit(solution)/shard_map/ppermute | solution.py:13
  33.8 3.5 collective-permute-done.5
  39.4 5.8 %collective-permute-done.6 = f32[2,1,16,128]{3,2,1,0:T(8,128)S(1)} collective-permute-done((f32[2,1,16,128]{3,2,1,0:T(8,128)S(1)}, f32[2,1,16,128]{3,2,1,0:T(8,128)S(1)}, u32[]{:S(2)}, u32[]{:S(2)}) %collective-permute-start.6) | collective-permute-done | bytes 16416 | tf_op jit(solution)/shard_map/ppermute | solution.py:13
  48.0 3.5 collective-permute-done.7
  53.5 5.8 %collective-permute-done.8 = f32[2,1,16,128]{3,2,1,0:T(8,128)S(1)} collective-permute-done((f32[2,1,16,128]{3,2,1,0:T(8,128)S(1)}, f32[2,1,16,128]{3,2,1,0:T(8,128)S(1)}, u32[]{:S(2)}, u32[]{:S(2)}) %collective-permute-start.8) | collective-permute-done | bytes 16416 | tf_op jit(solution)/shard_map/ppermute | solution.py:13
  60.8 3.7 collective-permute-done.9
  66.6 3.9 collective-permute-start.11
  70.5 3.8 collective-permute-done.11
  77.1 3.5 collective-permute-done.12
  82.6 5.8 %collective-permute-done.13 = f32[2,1,16,128]{3,2,1,0:T(8,128)S(1)} collective-permute-done((f32[2,1,16,128]{3,2,1,0:T(8,128)S(1)}, f32[2,1,16,128]{3,2,1,0:T(8,128)S(1)}, u32[]{:S(2)}, u32[]{:S(2)}) %collective-permute-start.13) | collective-permute-done | bytes 16416 | tf_op jit(solution)/shard_map/ppermute | solution.py:13
  98.3 4.3 collective-permute-done.15
  104.8 3.5 collective-permute-done.16
  110.2 5.8 %collective-permute-done.17 = f32[2,1,16,128]{3,2,1,0:T(8,128)S(1)} collective-permute-done((f32[2,1,16,128]{3,2,1,0:T(8,128)S(1)}, f32[2,1,16,128]{3,2,1,0:T(8,128)S(1)}, u32[]{:S(2)}, u32[]{:S(2)}) %collective-permute-start.17) | collective-permute-done | bytes 16416 | tf_op jit(solution)/shard_map/ppermute | solution.py:13
  118.2 6.0 %collective-permute-start.21 = (f32[64,1,16,128]{3,2,0,1:T(8,128)S(1)}, f32[64,1,16,128]{3,2,0,1:T(8,128)S(1)}, u32[]{:S(2)}, u32[]{:S(2)}) collective-permute-start(f32[64,1,16,128]{3,2,0,1:T(8,128)S(1)} %get-tuple-element.159), channel_id=1, source_target_pairs={{1,0},{2,1},{3,2},{4,3},{5,4},{6,5},{7,6},{8,7},{9,8},{10,9},{11,1... | collective-permute-start | bytes 1572872 | tf_op jit(solution)/shard_map/ppermute | solution.py:13
  126.6 3.9 collective-permute-start.20
  130.6 4.4 collective-permute-done.19
  135.1 9.6 %collective-permute-done.20 = f32[2,1,16,128]{3,2,1,0:T(8,128)S(1)} collective-permute-done((f32[2,1,16,128]{3,2,1,0:T(8,128)S(1)}, f32[2,1,16,128]{3,2,1,0:T(8,128)S(1)}, u32[]{:S(2)}, u32[]{:S(2)}) %collective-permute-start.20) | collective-permute-done | bytes 16416 | tf_op jit(solution)/shard_map/ppermute | solution.py:13
  151.9 6.0 %collective-permute-start.23 = (f32[64,1,16,128]{3,2,0,1:T(8,128)S(1)}, f32[64,1,16,128]{3,2,0,1:T(8,128)S(1)}, u32[]{:S(2)}, u32[]{:S(2)}) collective-permute-start(f32[64,1,16,128]{3,2,0,1:T(8,128)S(1)} %slice_bitcast_fusion.10), channel_id=1, source_target_pairs={{1,0},{2,1},{3,2},{4,3},{5,4},{6,5},{7,6},{8,7},{9,8},{10,9},{11,1... | collective-permute-start | bytes 1572872 | tf_op jit(solution)/shard_map/ppermute | solution.py:13
  158.4 20.7 %collective-permute-done.24 = f32[2,64,1,16,128]{4,3,1,2,0:T(8,128)S(1)} collective-permute-done((f32[2,64,1,16,128]{4,3,1,2,0:T(8,128)S(1)}, f32[2,64,1,16,128]{4,3,1,2,0:T(8,128)S(1)}, u32[]{:S(2)}, u32[]{:S(2)}) %collective-permute-start.24) | collective-permute-done | bytes 1048608 | tf_op jit(solution)/shard_map/ppermute | solution.py:13
  184.3 8.2 %fusion.10 = f32[64,64]{1,0:T(8,128)S(1)} fusion(f32[64,4,2,16,128]{4,3,2,1,0:T(8,128)S(1)} %bitcast.1043), kind=kOutput, calls=%fused_computation.12 | convolution fusion | flops 805306368 | bytes 4210688 | tf_op jit(solution)/shard_map/dot_general | solution.py:124
  193.6 9.3 %all-to-all-start = ((f32[16,1,4096]{2,1,0:T(1,128)}), f32[16,1,4096]{2,1,0:T(1,128)S(1)}, u32[]{:S(2)}, u32[]{:S(2)}) async-start(f32[16,1,4096]{2,1,0:T(1,128)} %reshape.1304), calls=%async_computation | async-start | bytes 524288 | tf_op jit(solution)/shard_map/all_to_all | solution.py:24
  202.9 5.0 %reshape_squeeze.3 = f32[64,16384]{1,0:T(8,128)} reshape(f32[1,64,4,2,16,128]{5,4,3,2,1,0:T(8,128)} %param.33) | data formatting | bytes 8388608 | tf_op jit(solution)/shard_map/reshape;squeeze | solution.py:123
  207.8 9.5 %all-to-all-done = f32[16,1,4096]{2,1,0:T(1,128)S(1)} async-done(((f32[16,1,4096]{2,1,0:T(1,128)}), f32[16,1,4096]{2,1,0:T(1,128)S(1)}, u32[]{:S(2)}, u32[]{:S(2)}) %all-to-all-start) | async-done | bytes 262176 | tf_op jit(solution)/shard_map/all_to_all | solution.py:24
  222.3 6.6 %cholesky.18 = f32[64,64]{1,0:T(8,128)S(1)} custom-call(f32[64,64]{1,0:T(8,128)} %fusion.69), custom_call_target="Cholesky" | custom-call | tf_op jit(solution)/shard_map/jit(cholesky)/cholesky | solution.py:125
  242.2 3.3 convolution_bitcast_fusion.13
  246.2 7.2 %all-to-all-start.1 = ((f32[16,1,64]{2,1,0:T(1,128)}), f32[16,1,64]{2,1,0:T(1,128)S(1)}, u32[]{:S(2)}, u32[]{:S(2)}) async-start(f32[16,1,64]{2,1,0:T(1,128)} %broadcast_in_dim.25), calls=%async_computation.1 | async-start | bytes 16384 | tf_op jit(solution)/shard_map/all_to_all | solution.py:24
  254.0 4.9 %custom-call.18 = f32[1,64,64]{1,2,0:T(8,128)S(1)} custom-call(f32[1,64,64]{2,1,0:T(8,128)S(1)} %fusion.57), custom_call_target="InvertDiagBlocksLowerTriangular" | custom-call | tf_op jit(solution)/shard_map/triangular_solve/custom-call.2 | solution.py:91
  258.9 9.3 %all-to-all-done.1 = f32[16,1,64]{2,1,0:T(1,128)S(1)} async-done(((f32[16,1,64]{2,1,0:T(1,128)}), f32[16,1,64]{2,1,0:T(1,128)S(1)}, u32[]{:S(2)}, u32[]{:S(2)}) %all-to-all-start.1) | async-done | bytes 4128 | tf_op jit(solution)/shard_map/all_to_all | solution.py:24
  268.3 4.1 collective-permute-start.27
  274.5 7.4 %collective-permute-done.27 = f32[64,1,16,128]{3,2,0,1:T(8,128)S(1)} collective-permute-done((f32[64,1,16,128]{3,2,0,1:T(8,128)S(1)}, f32[64,1,16,128]{3,2,0,1:T(8,128)S(1)}, u32[]{:S(2)}, u32[]{:S(2)}) %collective-permute-start.27) | collective-permute-done | bytes 524320 | tf_op jit(solution)/shard_map/ppermute | solution.py:13
  289.5 4.3 fusion.8
  293.9 3.7 collective-permute-done.29
  297.6 3.3 convolution_bitcast_fusion.12
  301.5 6.8 %all-to-all-start.2 = ((f32[16,1,64]{2,1,0:T(1,128)}), f32[16,1,64]{2,1,0:T(1,128)S(1)}, u32[]{:S(2)}, u32[]{:S(2)}) async-start(f32[16,1,64]{2,1,0:T(1,128)} %broadcast_in_dim.27), calls=%async_computation.2 | async-start | bytes 16384 | tf_op jit(solution)/shard_map/all_to_all | solution.py:24
  308.3 3.4 collective-permute-start.31
  311.7 4.8 %collective-permute-start.30 = (f32[1,16,128]{2,1,0:T(8,128)S(1)}, f32[1,16,128]{2,1,0:T(8,128)S(1)}, u32[]{:S(2)}, u32[]{:S(2)}) collective-permute-start(f32[1,16,128]{2,1,0:T(8,128)S(1)} %get-tuple-element.237), channel_id=1, source_target_pairs={{1,0},{2,1},{3,2},{4,3},{5,4},{6,5},{7,6},{8,7},{9,8},{10,9},{11,1... | collective-permute-start | bytes 24584 | tf_op jit(solution)/shard_map/ppermute | solution.py:13
  316.8 6.6 %fusion.6 = f32[1,4,2,16,128]{4,0,3,2,1:T(1,128)S(1)} fusion(f32[64,1,1,1,1]{0,1,4,3,2:T(1,128)S(1)} %convolution_bitcast_fusion.5, f32[4,2,16,128,64]{3,2,1,0,4:T(8,128)} %bitcast.1035), kind=kOutput, calls=%fused_computation.8 | convolution fusion | flops 12582912 | bytes 4260096 | tf_op jit(solution)/shard_map/dot_general | solution.py:133
  323.7 3.7 collective-permute-done.32
  331.3 5.1 %all-to-all-start.3 = ((f32[16,1,64]{2,1,0:T(1,128)}), f32[16,1,64]{2,1,0:T(1,128)S(1)}, u32[]{:S(2)}, u32[]{:S(2)}) async-start(f32[16,1,64]{2,1,0:T(1,128)} %broadcast_in_dim.29), calls=%async_computation.3 | async-start | bytes 16384 | tf_op jit(solution)/shard_map/all_to_all | solution.py:24
  336.5 3.4 collective-permute-start.34
  339.8 4.8 %collective-permute-start.33 = (f32[1,16,128]{2,1,0:T(8,128)S(1)}, f32[1,16,128]{2,1,0:T(8,128)S(1)}, u32[]{:S(2)}, u32[]{:S(2)}) collective-permute-start(f32[1,16,128]{2,1,0:T(8,128)S(1)} %get-tuple-element.228), channel_id=1, source_target_pairs={{1,0},{2,1},{3,2},{4,3},{5,4},{6,5},{7,6},{8,7},{9,8},{10,9},{11,1... | collective-permute-start | bytes 24584 | tf_op jit(solution)/shard_map/ppermute | solution.py:13
  345.0 6.6 %fusion.4 = f32[1,4,2,16,128]{4,0,3,2,1:T(1,128)S(1)} fusion(f32[64,1,1,1,1]{0,1,4,3,2:T(1,128)S(1)} %convolution_bitcast_fusion.3, f32[4,2,16,128,64]{3,2,1,0,4:T(8,128)} %bitcast.1036), kind=kOutput, calls=%fused_computation.6 | convolution fusion | flops 12582912 | bytes 4260096 | tf_op jit(solution)/shard_map/dot_general | solution.py:133
  353.2 6.4 %collective-permute-done.35 = f32[4,2,16,128]{3,2,1,0:T(8,128)S(1)} collective-permute-done((f32[4,2,16,128]{3,2,1,0:T(8,128)S(1)}, f32[4,2,16,128]{3,2,1,0:T(8,128)S(1)}, u32[]{:S(2)}, u32[]{:S(2)}) %collective-permute-start.35) | collective-permute-done | bytes 65568 | tf_op jit(solution)/shard_map/ppermute | solution.py:13
  362.1 3.4 collective-permute-start.37
  365.5 4.3 collective-permute-done.37
  372.0 6.0 %collective-permute-start.38 = (f32[1,16,128]{2,1,0:T(8,128)S(1)}, f32[1,16,128]{2,1,0:T(8,128)S(1)}, u32[]{:S(2)}, u32[]{:S(2)}) collective-permute-start(f32[1,16,128]{2,1,0:T(8,128)S(1)} %slice_bitcast_fusion.56), channel_id=1, source_target_pairs={{1,0},{2,1},{3,2},{4,3},{5,4},{6,5},{7,6},{8,7},{9,8},{10,9},{11,1... | collective-permute-start | bytes 24584 | tf_op jit(solution)/shard_map/ppermute | solution.py:13
  379.5 3.7 collective-permute-done.40
  387.1 8.7 %all-to-all-start.4 = ((f32[16,1,64]{2,1,0:T(1,128)}), f32[16,1,64]{2,1,0:T(1,128)S(1)}, u32[]{:S(2)}, u32[]{:S(2)}) async-start(f32[16,1,64]{2,1,0:T(1,128)} %broadcast_in_dim.31), calls=%async_computation.4 | async-start | bytes 16384 | tf_op jit(solution)/shard_map/all_to_all | solution.py:24
  395.8 3.4 collective-permute-start.42
  399.2 4.8 %collective-permute-start.41 = (f32[1,16,128]{2,1,0:T(8,128)S(1)}, f32[1,16,128]{2,1,0:T(8,128)S(1)}, u32[]{:S(2)}, u32[]{:S(2)}) collective-permute-start(f32[1,16,128]{2,1,0:T(8,128)S(1)} %get-tuple-element.209), channel_id=1, source_target_pairs={{1,0},{2,1},{3,2},{4,3},{5,4},{6,5},{7,6},{8,7},{9,8},{10,9},{11,1... | collective-permute-start | bytes 24584 | tf_op jit(solution)/shard_map/ppermute | solution.py:13
  404.4 6.6 %fusion.2 = f32[1,4,2,16,128]{4,0,3,2,1:T(1,128)S(1)} fusion(f32[64,1,1,1,1]{0,1,4,3,2:T(1,128)S(1)} %convolution_bitcast_fusion.1, f32[4,2,16,128,64]{3,2,1,0,4:T(8,128)} %bitcast.1037), kind=kOutput, calls=%fused_computation.4 | convolution fusion | flops 12582912 | bytes 4260096 | tf_op jit(solution)/shard_map/dot_general | solution.py:133
  411.2 3.3 convolution_bitcast_fusion.9
  415.2 5.1 %all-to-all-start.5 = ((f32[16,1,64]{2,1,0:T(1,128)}), f32[16,1,64]{2,1,0:T(1,128)S(1)}, u32[]{:S(2)}, u32[]{:S(2)}) async-start(f32[16,1,64]{2,1,0:T(1,128)} %broadcast_in_dim.33), calls=%async_computation.5 | async-start | bytes 16384 | tf_op jit(solution)/shard_map/all_to_all | solution.py:24
  420.3 6.1 %all-to-all-done.5 = f32[16,1,64]{2,1,0:T(1,128)S(1)} async-done(((f32[16,1,64]{2,1,0:T(1,128)}), f32[16,1,64]{2,1,0:T(1,128)S(1)}, u32[]{:S(2)}, u32[]{:S(2)}) %all-to-all-start.5) | async-done | bytes 4128 | tf_op jit(solution)/shard_map/all_to_all | solution.py:24
  427.3 4.0 collective-permute-start.44
  433.4 5.7 %collective-permute-done.45 = f32[2,1,16,128]{3,2,1,0:T(8,128)S(1)} collective-permute-done((f32[2,1,16,128]{3,2,1,0:T(8,128)S(1)}, f32[2,1,16,128]{3,2,1,0:T(8,128)S(1)}, u32[]{:S(2)}, u32[]{:S(2)}) %collective-permute-start.45) | collective-permute-done | bytes 16416 | tf_op jit(solution)/shard_map/ppermute | solution.py:13
  441.2 3.9 collective-permute-start.47
  445.2 3.8 collective-permute-done.47
  451.1 3.9 collective-permute-start.49
  455.1 3.8 collective-permute-done.49
  (360 shorter events, 112.2 us)
Async XLA Ops:
  0.6 3.9 collective-permute-start
  4.5 6.5 %collective-permute-start.1 = (f32[1,16,128]{2,1,0:T(8,128)S(1)}, f32[1,16,128]{2,1,0:T(8,128)S(1)}, u32[]{:S(2)}, u32[]{:S(2)}) collective-permute-start(f32[1,16,128]{2,1,0:T(8,128)S(1)} %get-tuple-element.266), channel_id=1, source_target_pairs={{1,0},{2,1},{3,2},{4,3},{5,4},{6,5},{7,6},{8,7},{9,8},{10,9},{11,1... | collective-permute-start | bytes 24584 | tf_op jit(solution)/shard_map/ppermute | solution.py:13
  9.1 7.7 %collective-permute-start.2 = (f32[2,1,16,128]{3,2,1,0:T(8,128)S(1)}, f32[2,1,16,128]{3,2,1,0:T(8,128)S(1)}, u32[]{:S(2)}, u32[]{:S(2)}) collective-permute-start(f32[2,1,16,128]{3,2,1,0:T(8,128)S(1)} %pad_maximum_fusion.9), channel_id=1, source_target_pairs={{0,1},{1,2},{2,3},{3,4},{4,5},{5,6},{6,7},{7,8},{8,9},{9,10},{10,1... | collective-permute-start | bytes 49160 | tf_op jit(solution)/shard_map/ppermute | solution.py:13
  17.7 5.5 %collective-permute-start.3 = (f32[1,16,128]{2,1,0:T(8,128)S(1)}, f32[1,16,128]{2,1,0:T(8,128)S(1)}, u32[]{:S(2)}, u32[]{:S(2)}) collective-permute-start(f32[1,16,128]{2,1,0:T(8,128)S(1)} %get-tuple-element.322), channel_id=1, source_target_pairs={{1,0},{2,1},{3,2},{4,3},{5,4},{6,5},{7,6},{8,7},{9,8},{10,9},{11,1... | collective-permute-start | bytes 24584 | tf_op jit(solution)/shard_map/ppermute | solution.py:13
  23.3 7.7 %collective-permute-start.4 = (f32[2,1,16,128]{3,2,1,0:T(8,128)S(1)}, f32[2,1,16,128]{3,2,1,0:T(8,128)S(1)}, u32[]{:S(2)}, u32[]{:S(2)}) collective-permute-start(f32[2,1,16,128]{3,2,1,0:T(8,128)S(1)} %pad_maximum_fusion.10), channel_id=1, source_target_pairs={{0,1},{1,2},{2,3},{3,4},{4,5},{5,6},{6,7},{7,8},{8,9},{9,10},{10,1... | collective-permute-start | bytes 49160 | tf_op jit(solution)/shard_map/ppermute | solution.py:13
  31.8 5.5 %collective-permute-start.5 = (f32[1,16,128]{2,1,0:T(8,128)S(1)}, f32[1,16,128]{2,1,0:T(8,128)S(1)}, u32[]{:S(2)}, u32[]{:S(2)}) collective-permute-start(f32[1,16,128]{2,1,0:T(8,128)S(1)} %get-tuple-element.315), channel_id=1, source_target_pairs={{1,0},{2,1},{3,2},{4,3},{5,4},{6,5},{7,6},{8,7},{9,8},{10,9},{11,1... | collective-permute-start | bytes 24584 | tf_op jit(solution)/shard_map/ppermute | solution.py:13
  37.4 7.7 %collective-permute-start.6 = (f32[2,1,16,128]{3,2,1,0:T(8,128)S(1)}, f32[2,1,16,128]{3,2,1,0:T(8,128)S(1)}, u32[]{:S(2)}, u32[]{:S(2)}) collective-permute-start(f32[2,1,16,128]{3,2,1,0:T(8,128)S(1)} %pad_maximum_fusion.11), channel_id=1, source_target_pairs={{0,1},{1,2},{2,3},{3,4},{4,5},{5,6},{6,7},{7,8},{8,9},{9,10},{10,1... | collective-permute-start | bytes 49160 | tf_op jit(solution)/shard_map/ppermute | solution.py:13
  46.0 5.5 %collective-permute-start.7 = (f32[1,16,128]{2,1,0:T(8,128)S(1)}, f32[1,16,128]{2,1,0:T(8,128)S(1)}, u32[]{:S(2)}, u32[]{:S(2)}) collective-permute-start(f32[1,16,128]{2,1,0:T(8,128)S(1)} %get-tuple-element.308), channel_id=1, source_target_pairs={{1,0},{2,1},{3,2},{4,3},{5,4},{6,5},{7,6},{8,7},{9,8},{10,9},{11,1... | collective-permute-start | bytes 24584 | tf_op jit(solution)/shard_map/ppermute | solution.py:13
  51.6 7.7 %collective-permute-start.8 = (f32[2,1,16,128]{3,2,1,0:T(8,128)S(1)}, f32[2,1,16,128]{3,2,1,0:T(8,128)S(1)}, u32[]{:S(2)}, u32[]{:S(2)}) collective-permute-start(f32[2,1,16,128]{3,2,1,0:T(8,128)S(1)} %pad_maximum_fusion.12), channel_id=1, source_target_pairs={{0,1},{1,2},{2,3},{3,4},{4,5},{5,6},{6,7},{7,8},{8,9},{9,10},{10,1... | collective-permute-start | bytes 49160 | tf_op jit(solution)/shard_map/ppermute | solution.py:13
  60.8 3.7 collective-permute-start.9
  64.5 5.9 %collective-permute-start.10 = (f32[1,16,128]{2,1,0:T(8,128)S(1)}, f32[1,16,128]{2,1,0:T(8,128)S(1)}, u32[]{:S(2)}, u32[]{:S(2)}) collective-permute-start(f32[1,16,128]{2,1,0:T(8,128)S(1)} %get-tuple-element.259), channel_id=1, source_target_pairs={{1,0},{2,1},{3,2},{4,3},{5,4},{6,5},{7,6},{8,7},{9,8},{10,9},{11,1... | collective-permute-start | bytes 24584 | tf_op jit(solution)/shard_map/ppermute | solution.py:13
  66.6 7.7 %collective-permute-start.11 = (f32[2,1,16,128]{3,2,1,0:T(8,128)S(1)}, f32[2,1,16,128]{3,2,1,0:T(8,128)S(1)}, u32[]{:S(2)}, u32[]{:S(2)}) collective-permute-start(f32[2,1,16,128]{3,2,1,0:T(8,128)S(1)} %pad_maximum_fusion.13), channel_id=1, source_target_pairs={{0,1},{1,2},{2,3},{3,4},{4,5},{5,6},{6,7},{7,8},{8,9},{9,10},{10,1... | collective-permute-start | bytes 49160 | tf_op jit(solution)/shard_map/ppermute | solution.py:13
  75.1 5.5 %collective-permute-start.12 = (f32[1,16,128]{2,1,0:T(8,128)S(1)}, f32[1,16,128]{2,1,0:T(8,128)S(1)}, u32[]{:S(2)}, u32[]{:S(2)}) collective-permute-start(f32[1,16,128]{2,1,0:T(8,128)S(1)} %get-tuple-element.301), channel_id=1, source_target_pairs={{1,0},{2,1},{3,2},{4,3},{5,4},{6,5},{7,6},{8,7},{9,8},{10,9},{11,1... | collective-permute-start | bytes 24584 | tf_op jit(solution)/shard_map/ppermute | solution.py:13
  80.7 7.7 %collective-permute-start.13 = (f32[2,1,16,128]{3,2,1,0:T(8,128)S(1)}, f32[2,1,16,128]{3,2,1,0:T(8,128)S(1)}, u32[]{:S(2)}, u32[]{:S(2)}) collective-permute-start(f32[2,1,16,128]{3,2,1,0:T(8,128)S(1)} %pad_maximum_fusion.14), channel_id=1, source_target_pairs={{0,1},{1,2},{2,3},{3,4},{4,5},{5,6},{6,7},{7,8},{8,9},{9,10},{10,1... | collective-permute-start | bytes 49160 | tf_op jit(solution)/shard_map/ppermute | solution.py:13
  89.3 5.5 %collective-permute-start.14 = (f32[1,16,128]{2,1,0:T(8,128)S(1)}, f32[1,16,128]{2,1,0:T(8,128)S(1)}, u32[]{:S(2)}, u32[]{:S(2)}) collective-permute-start(f32[1,16,128]{2,1,0:T(8,128)S(1)} %get-tuple-element.294), channel_id=1, source_target_pairs={{1,0},{2,1},{3,2},{4,3},{5,4},{6,5},{7,6},{8,7},{9,8},{10,9},{11,1... | collective-permute-start | bytes 24584 | tf_op jit(solution)/shard_map/ppermute | solution.py:13
  94.0 8.6 %copy-start.17 = (f32[2,16,128]{2,1,0:T(8,128)S(1)}, f32[2,16,128]{2,1,0:T(8,128)}, u32[]{:S(2)}) copy-start(f32[2,16,128]{2,1,0:T(8,128)} %param.30) | copy-start | bytes 49156
  94.0 8.6 %copy-start.21 = (f32[4,2,16,128]{3,2,1,0:T(8,128)S(1)}, f32[4,2,16,128]{3,2,1,0:T(8,128)}, u32[]{:S(2)}) copy-start(f32[4,2,16,128]{3,2,1,0:T(8,128)} %param.31) | copy-start | bytes 196612
  94.9 7.7 %collective-permute-start.15 = (f32[2,1,16,128]{3,2,1,0:T(8,128)S(1)}, f32[2,1,16,128]{3,2,1,0:T(8,128)S(1)}, u32[]{:S(2)}, u32[]{:S(2)}) collective-permute-start(f32[2,1,16,128]{3,2,1,0:T(8,128)S(1)} %pad_maximum_fusion.15), channel_id=1, source_target_pairs={{0,1},{1,2},{2,3},{3,4},{4,5},{5,6},{6,7},{7,8},{8,9},{9,10},{10,1... | collective-permute-start | bytes 49160 | tf_op jit(solution)/shard_map/ppermute | solution.py:13
  102.7 5.5 %collective-permute-start.16 = (f32[1,16,128]{2,1,0:T(8,128)S(1)}, f32[1,16,128]{2,1,0:T(8,128)S(1)}, u32[]{:S(2)}, u32[]{:S(2)}) collective-permute-start(f32[1,16,128]{2,1,0:T(8,128)S(1)} %get-tuple-element.287), channel_id=1, source_target_pairs={{1,0},{2,1},{3,2},{4,3},{5,4},{6,5},{7,6},{8,7},{9,8},{10,9},{11,1... | collective-permute-start | bytes 24584 | tf_op jit(solution)/shard_map/ppermute | solution.py:13
  108.3 7.7 %collective-permute-start.17 = (f32[2,1,16,128]{3,2,1,0:T(8,128)S(1)}, f32[2,1,16,128]{3,2,1,0:T(8,128)S(1)}, u32[]{:S(2)}, u32[]{:S(2)}) collective-permute-start(f32[2,1,16,128]{3,2,1,0:T(8,128)S(1)} %pad_maximum_fusion.16), channel_id=1, source_target_pairs={{0,1},{1,2},{2,3},{3,4},{4,5},{5,6},{6,7},{7,8},{8,9},{9,10},{10,1... | collective-permute-start | bytes 49160 | tf_op jit(solution)/shard_map/ppermute | solution.py:13
  116.2 8.5 %collective-permute-start.18 = (f32[4,2,16,128]{3,2,1,0:T(8,128)S(1)}, f32[4,2,16,128]{3,2,1,0:T(8,128)S(1)}, u32[]{:S(2)}, u32[]{:S(2)}) collective-permute-start(f32[4,2,16,128]{3,2,1,0:T(8,128)S(1)} %sub.1271), channel_id=1, source_target_pairs={{0,16},{16,32},{32,48},{48,64},{64,80},{80,96},{96,112},{112,0},{1... | collective-permute-start | bytes 196616 | tf_op jit(solution)/shard_map/ppermute | solution.py:19
  116.3 29.0 %collective-permute-start.22 = (f32[2,64,1,16,128]{4,3,1,2,0:T(8,128)S(1)}, f32[2,64,1,16,128]{4,3,1,2,0:T(8,128)S(1)}, u32[]{:S(2)}, u32[]{:S(2)}) collective-permute-start(f32[2,64,1,16,128]{4,3,1,2,0:T(8,128)S(1)} %pad_maximum_fusion), channel_id=1, source_target_pairs={{0,1},{1,2},{2,3},{3,4},{4,5},{5,6},{6,7},{7,8},{8,9},{9,10},{10,1... | collective-permute-start | bytes 3145736 | tf_op jit(solution)/shard_map/ppermute | solution.py:13
  118.2 27.3 %collective-permute-start.21 = (f32[64,1,16,128]{3,2,0,1:T(8,128)S(1)}, f32[64,1,16,128]{3,2,0,1:T(8,128)S(1)}, u32[]{:S(2)}, u32[]{:S(2)}) collective-permute-start(f32[64,1,16,128]{3,2,0,1:T(8,128)S(1)} %get-tuple-element.159), channel_id=1, source_target_pairs={{1,0},{2,1},{3,2},{4,3},{5,4},{6,5},{7,6},{8,7},{9,8},{10,9},{11,1... | collective-permute-start | bytes 1572872 | tf_op jit(solution)/shard_map/ppermute | solution.py:13
  124.7 10.3 %collective-permute-start.19 = (f32[1,16,128]{2,1,0:T(8,128)S(1)}, f32[1,16,128]{2,1,0:T(8,128)S(1)}, u32[]{:S(2)}, u32[]{:S(2)}) collective-permute-start(f32[1,16,128]{2,1,0:T(8,128)S(1)} %get-tuple-element.246), channel_id=1, source_target_pairs={{1,0},{2,1},{3,2},{4,3},{5,4},{6,5},{7,6},{8,7},{9,8},{10,9},{11,1... | collective-permute-start | bytes 24584 | tf_op jit(solution)/shard_map/ppermute | solution.py:13
  126.6 18.0 %collective-permute-start.20 = (f32[2,1,16,128]{3,2,1,0:T(8,128)S(1)}, f32[2,1,16,128]{3,2,1,0:T(8,128)S(1)}, u32[]{:S(2)}, u32[]{:S(2)}) collective-permute-start(f32[2,1,16,128]{3,2,1,0:T(8,128)S(1)} %pad_maximum_fusion.17), channel_id=1, source_target_pairs={{0,1},{1,2},{2,3},{3,4},{4,5},{5,6},{6,7},{7,8},{8,9},{9,10},{10,1... | collective-permute-start | bytes 49160 | tf_op jit(solution)/shard_map/ppermute | solution.py:13
  149.9 29.2 %collective-permute-start.24 = (f32[2,64,1,16,128]{4,3,1,2,0:T(8,128)S(1)}, f32[2,64,1,16,128]{4,3,1,2,0:T(8,128)S(1)}, u32[]{:S(2)}, u32[]{:S(2)}) collective-permute-start(f32[2,64,1,16,128]{4,3,1,2,0:T(8,128)S(1)} %pad_maximum_fusion.1), channel_id=1, source_target_pairs={{0,1},{1,2},{2,3},{3,4},{4,5},{5,6},{6,7},{7,8},{8,9},{9,10},{10,1... | collective-permute-start | bytes 3145736 | tf_op jit(solution)/shard_map/ppermute | solution.py:13
  151.9 27.3 %collective-permute-start.23 = (f32[64,1,16,128]{3,2,0,1:T(8,128)S(1)}, f32[64,1,16,128]{3,2,0,1:T(8,128)S(1)}, u32[]{:S(2)}, u32[]{:S(2)}) collective-permute-start(f32[64,1,16,128]{3,2,0,1:T(8,128)S(1)} %slice_bitcast_fusion.10), channel_id=1, source_target_pairs={{1,0},{2,1},{3,2},{4,3},{5,4},{6,5},{7,6},{8,7},{9,8},{10,9},{11,1... | collective-permute-start | bytes 1572872 | tf_op jit(solution)/shard_map/ppermute | solution.py:13
  182.2 47.8 %collective-permute-start.26 = (f32[2,64,1,16,128]{4,3,1,2,0:T(8,128)}, f32[2,64,1,16,128]{4,3,1,2,0:T(8,128)}, u32[]{:S(2)}, u32[]{:S(2)}) collective-permute-start(f32[2,64,1,16,128]{4,3,1,2,0:T(8,128)} %pad_maximum_fusion.2), channel_id=1, source_target_pairs={{0,1},{1,2},{2,3},{3,4},{4,5},{5,6},{6,7},{7,8},{8,9},{9,10},{10,1... | collective-permute-start | bytes 3145736 | tf_op jit(solution)/shard_map/ppermute | solution.py:13
  193.6 23.8 %all-to-all-start = ((f32[16,1,4096]{2,1,0:T(1,128)}), f32[16,1,4096]{2,1,0:T(1,128)S(1)}, u32[]{:S(2)}, u32[]{:S(2)}) async-start(f32[16,1,4096]{2,1,0:T(1,128)} %reshape.1304), calls=%async_computation | async-start | bytes 524288 | tf_op jit(solution)/shard_map/all_to_all | solution.py:24
  219.6 15.1 %collective-permute-start.25 = (f32[64,1,16,128]{3,2,0,1:T(8,128)S(1)}, f32[64,1,16,128]{3,2,0,1:T(8,128)S(1)}, u32[]{:S(2)}, u32[]{:S(2)}) collective-permute-start(f32[64,1,16,128]{3,2,0,1:T(8,128)S(1)} %slice_bitcast_fusion.7), channel_id=1, source_target_pairs={{1,0},{2,1},{3,2},{4,3},{5,4},{6,5},{7,6},{8,7},{9,8},{10,9},{11,1... | collective-permute-start | bytes 1572872 | tf_op jit(solution)/shard_map/ppermute | solution.py:13
  240.1 33.0 %collective-permute-start.28 = (f32[2,64,1,16,128]{4,3,1,2,0:T(8,128)}, f32[2,64,1,16,128]{4,3,1,2,0:T(8,128)}, u32[]{:S(2)}, u32[]{:S(2)}) collective-permute-start(f32[2,64,1,16,128]{4,3,1,2,0:T(8,128)} %pad_maximum_fusion.3), channel_id=1, source_target_pairs={{0,1},{1,2},{2,3},{3,4},{4,5},{5,6},{6,7},{7,8},{8,9},{9,10},{10,1... | collective-permute-start | bytes 3145736 | tf_op jit(solution)/shard_map/ppermute | solution.py:13
  246.2 22.1 %all-to-all-start.1 = ((f32[16,1,64]{2,1,0:T(1,128)}), f32[16,1,64]{2,1,0:T(1,128)S(1)}, u32[]{:S(2)}, u32[]{:S(2)}) async-start(f32[16,1,64]{2,1,0:T(1,128)} %broadcast_in_dim.25), calls=%async_computation.1 | async-start | bytes 16384 | tf_op jit(solution)/shard_map/all_to_all | solution.py:24
  268.2 13.7 %copy-start.10 = (f32[64,2,16,128]{3,2,0,1:T(8,128)S(1)}, f32[64,2,16,128]{3,2,0,1:T(8,128)}, u32[]{:S(2)}) copy-start(f32[64,2,16,128]{3,2,0,1:T(8,128)} %copy-done.9) | copy-start | bytes 3145732
  268.3 13.7 %copy-start.12 = (f32[64,2,16,128]{3,2,0,1:T(8,128)S(1)}, f32[64,2,16,128]{3,2,0,1:T(8,128)}, u32[]{:S(2)}) copy-start(f32[64,2,16,128]{3,2,0,1:T(8,128)} %copy-done.11) | copy-start | bytes 3145732
  268.3 13.6 %collective-permute-start.27 = (f32[64,1,16,128]{3,2,0,1:T(8,128)S(1)}, f32[64,1,16,128]{3,2,0,1:T(8,128)S(1)}, u32[]{:S(2)}, u32[]{:S(2)}) collective-permute-start(f32[64,1,16,128]{3,2,0,1:T(8,128)S(1)} %slice_bitcast_fusion.3), channel_id=1, source_target_pairs={{1,0},{2,1},{3,2},{4,3},{5,4},{6,5},{7,6},{8,7},{9,8},{10,9},{11,1... | collective-permute-start | bytes 1572872 | tf_op jit(solution)/shard_map/ppermute | solution.py:13
  289.4 11.5 %copy-start.5 = (f32[8,8,128,128]{3,2,1,0:T(8,128)}, f32[8,8,128,128]{3,2,1,0:T(8,128)S(1)}, u32[]{:S(2)}) copy-start(f32[8,8,128,128]{3,2,1,0:T(8,128)S(1)} %copy.62) | copy-start | bytes 12582916
  289.5 8.1 %copy-start.1 = (f32[64,16384]{1,0:T(8,128)S(1)}, f32[64,16384]{1,0:T(8,128)}, u32[]{:S(2)}) copy-start(f32[64,16384]{1,0:T(8,128)} %reshape_squeeze.3) | copy-start | bytes 12582916
  293.8 3.7 collective-permute-start.29
  301.5 14.9 %all-to-all-start.2 = ((f32[16,1,64]{2,1,0:T(1,128)}), f32[16,1,64]{2,1,0:T(1,128)S(1)}, u32[]{:S(2)}, u32[]{:S(2)}) async-start(f32[16,1,64]{2,1,0:T(1,128)} %broadcast_in_dim.27), calls=%async_computation.2 | async-start | bytes 16384 | tf_op jit(solution)/shard_map/all_to_all | solution.py:24
  308.3 15.2 %collective-permute-start.31 = (f32[2,1,16,128]{3,2,1,0:T(8,128)S(1)}, f32[2,1,16,128]{3,2,1,0:T(8,128)S(1)}, u32[]{:S(2)}, u32[]{:S(2)}) collective-permute-start(f32[2,1,16,128]{3,2,1,0:T(8,128)S(1)} %pad_maximum_fusion.18), channel_id=1, source_target_pairs={{0,1},{1,2},{2,3},{3,4},{4,5},{5,6},{6,7},{7,8},{8,9},{9,10},{10,1... | collective-permute-start | bytes 49160 | tf_op jit(solution)/shard_map/ppermute | solution.py:13
  311.7 11.7 %collective-permute-start.30 = (f32[1,16,128]{2,1,0:T(8,128)S(1)}, f32[1,16,128]{2,1,0:T(8,128)S(1)}, u32[]{:S(2)}, u32[]{:S(2)}) collective-permute-start(f32[1,16,128]{2,1,0:T(8,128)S(1)} %get-tuple-element.237), channel_id=1, source_target_pairs={{1,0},{2,1},{3,2},{4,3},{5,4},{6,5},{7,6},{8,7},{9,8},{10,9},{11,1... | collective-permute-start | bytes 24584 | tf_op jit(solution)/shard_map/ppermute | solution.py:13
  316.5 10.9 %copy-start.2 = (f32[64,16384]{1,0:T(8,128)S(1)}, f32[64,16384]{1,0:T(8,128)}, u32[]{:S(2)}) copy-start(f32[64,16384]{1,0:T(8,128)} %reshape_squeeze.3) | copy-start | bytes 12582916
  323.7 3.7 collective-permute-start.32
  331.3 13.3 %all-to-all-start.3 = ((f32[16,1,64]{2,1,0:T(1,128)}), f32[16,1,64]{2,1,0:T(1,128)S(1)}, u32[]{:S(2)}, u32[]{:S(2)}) async-start(f32[16,1,64]{2,1,0:T(1,128)} %broadcast_in_dim.29), calls=%async_computation.3 | async-start | bytes 16384 | tf_op jit(solution)/shard_map/all_to_all | solution.py:24
  336.5 15.3 %collective-permute-start.34 = (f32[2,1,16,128]{3,2,1,0:T(8,128)S(1)}, f32[2,1,16,128]{3,2,1,0:T(8,128)S(1)}, u32[]{:S(2)}, u32[]{:S(2)}) collective-permute-start(f32[2,1,16,128]{3,2,1,0:T(8,128)S(1)} %pad_maximum_fusion.19), channel_id=1, source_target_pairs={{0,1},{1,2},{2,3},{3,4},{4,5},{5,6},{6,7},{7,8},{8,9},{9,10},{10,1... | collective-permute-start | bytes 49160 | tf_op jit(solution)/shard_map/ppermute | solution.py:13
  339.8 11.7 %collective-permute-start.33 = (f32[1,16,128]{2,1,0:T(8,128)S(1)}, f32[1,16,128]{2,1,0:T(8,128)S(1)}, u32[]{:S(2)}, u32[]{:S(2)}) collective-permute-start(f32[1,16,128]{2,1,0:T(8,128)S(1)} %get-tuple-element.228), channel_id=1, source_target_pairs={{1,0},{2,1},{3,2},{4,3},{5,4},{6,5},{7,6},{8,7},{9,8},{10,9},{11,1... | collective-permute-start | bytes 24584 | tf_op jit(solution)/shard_map/ppermute | solution.py:13
  344.7 38.5 %copy-start.3 = (f32[64,16384]{1,0:T(8,128)S(1)}, f32[64,16384]{1,0:T(8,128)}, u32[]{:S(2)}) copy-start(f32[64,16384]{1,0:T(8,128)} %reshape_squeeze.3) | copy-start | bytes 12582916
  351.9 7.7 %collective-permute-start.35 = (f32[4,2,16,128]{3,2,1,0:T(8,128)S(1)}, f32[4,2,16,128]{3,2,1,0:T(8,128)S(1)}, u32[]{:S(2)}, u32[]{:S(2)}) collective-permute-start(f32[4,2,16,128]{3,2,1,0:T(8,128)S(1)} %fusion.53), channel_id=1, source_target_pairs={{0,64},{16,80},{32,96},{48,112},{1,65},{17,81},{33,97},{49,113},{2... | collective-permute-start | bytes 196616 | tf_op jit(solution)/shard_map/ppermute | solution.py:13
  359.5 6.0 %collective-permute-start.36 = (f32[1,16,128]{2,1,0:T(8,128)S(1)}, f32[1,16,128]{2,1,0:T(8,128)S(1)}, u32[]{:S(2)}, u32[]{:S(2)}) collective-permute-start(f32[1,16,128]{2,1,0:T(8,128)S(1)} %get-tuple-element.225), channel_id=1, source_target_pairs={{1,0},{2,1},{3,2},{4,3},{5,4},{6,5},{7,6},{8,7},{9,8},{10,9},{11,1... | collective-permute-start | bytes 24584 | tf_op jit(solution)/shard_map/ppermute | solution.py:13
  362.1 7.7 %collective-permute-start.37 = (f32[2,1,16,128]{3,2,1,0:T(8,128)S(1)}, f32[2,1,16,128]{3,2,1,0:T(8,128)S(1)}, u32[]{:S(2)}, u32[]{:S(2)}) collective-permute-start(f32[2,1,16,128]{3,2,1,0:T(8,128)S(1)} %pad_maximum_fusion.20), channel_id=1, source_target_pairs={{0,1},{1,2},{2,3},{3,4},{4,5},{5,6},{6,7},{7,8},{8,9},{9,10},{10,1... | collective-permute-start | bytes 49160 | tf_op jit(solution)/shard_map/ppermute | solution.py:13
  369.9 8.0 %collective-permute-start.39 = (f32[2,1,16,128]{3,2,1,0:T(8,128)S(1)}, f32[2,1,16,128]{3,2,1,0:T(8,128)S(1)}, u32[]{:S(2)}, u32[]{:S(2)}) collective-permute-start(f32[2,1,16,128]{3,2,1,0:T(8,128)S(1)} %pad_maximum_fusion.21), channel_id=1, source_target_pairs={{0,1},{1,2},{2,3},{3,4},{4,5},{5,6},{6,7},{7,8},{8,9},{9,10},{10,1... | collective-permute-start | bytes 49160 | tf_op jit(solution)/shard_map/ppermute | solution.py:13
  372.0 7.4 %collective-permute-start.38 = (f32[1,16,128]{2,1,0:T(8,128)S(1)}, f32[1,16,128]{2,1,0:T(8,128)S(1)}, u32[]{:S(2)}, u32[]{:S(2)}) collective-permute-start(f32[1,16,128]{2,1,0:T(8,128)S(1)} %slice_bitcast_fusion.56), channel_id=1, source_target_pairs={{1,0},{2,1},{3,2},{4,3},{5,4},{6,5},{7,6},{8,7},{9,8},{10,9},{11,1... | collective-permute-start | bytes 24584 | tf_op jit(solution)/shard_map/ppermute | solution.py:13
  379.5 3.7 collective-permute-start.40
  387.1 16.9 %all-to-all-start.4 = ((f32[16,1,64]{2,1,0:T(1,128)}), f32[16,1,64]{2,1,0:T(1,128)S(1)}, u32[]{:S(2)}, u32[]{:S(2)}) async-start(f32[16,1,64]{2,1,0:T(1,128)} %broadcast_in_dim.31), calls=%async_computation.4 | async-start | bytes 16384 | tf_op jit(solution)/shard_map/all_to_all | solution.py:24
  395.8 15.3 %collective-permute-start.42 = (f32[2,1,16,128]{3,2,1,0:T(8,128)S(1)}, f32[2,1,16,128]{3,2,1,0:T(8,128)S(1)}, u32[]{:S(2)}, u32[]{:S(2)}) collective-permute-start(f32[2,1,16,128]{3,2,1,0:T(8,128)S(1)} %pad_maximum_fusion.22), channel_id=1, source_target_pairs={{0,1},{1,2},{2,3},{3,4},{4,5},{5,6},{6,7},{7,8},{8,9},{9,10},{10,1... | collective-permute-start | bytes 49160 | tf_op jit(solution)/shard_map/ppermute | solution.py:13
  399.2 11.8 %collective-permute-start.41 = (f32[1,16,128]{2,1,0:T(8,128)S(1)}, f32[1,16,128]{2,1,0:T(8,128)S(1)}, u32[]{:S(2)}, u32[]{:S(2)}) collective-permute-start(f32[1,16,128]{2,1,0:T(8,128)S(1)} %get-tuple-element.209), channel_id=1, source_target_pairs={{1,0},{2,1},{3,2},{4,3},{5,4},{6,5},{7,6},{8,7},{9,8},{10,9},{11,1... | collective-permute-start | bytes 24584 | tf_op jit(solution)/shard_map/ppermute | solution.py:13
  415.2 11.3 %all-to-all-start.5 = ((f32[16,1,64]{2,1,0:T(1,128)}), f32[16,1,64]{2,1,0:T(1,128)S(1)}, u32[]{:S(2)}, u32[]{:S(2)}) async-start(f32[16,1,64]{2,1,0:T(1,128)} %broadcast_in_dim.33), calls=%async_computation.5 | async-start | bytes 16384 | tf_op jit(solution)/shard_map/all_to_all | solution.py:24
  420.3 7.0 %collective-permute-start.43 = (f32[4,2,16,128]{3,2,1,0:T(8,128)S(1)}, f32[4,2,16,128]{3,2,1,0:T(8,128)S(1)}, u32[]{:S(2)}, u32[]{:S(2)}) collective-permute-start(f32[4,2,16,128]{3,2,1,0:T(8,128)S(1)} %fusion.56), channel_id=1, source_target_pairs={{0,16},{16,32},{32,48},{48,64},{64,80},{80,96},{96,112},{112,0},{1... | collective-permute-start | bytes 196616 | tf_op jit(solution)/shard_map/ppermute | solution.py:19
  427.3 5.9 %collective-permute-start.44 = (f32[1,16,128]{2,1,0:T(8,128)S(1)}, f32[1,16,128]{2,1,0:T(8,128)S(1)}, u32[]{:S(2)}, u32[]{:S(2)}) collective-permute-start(f32[1,16,128]{2,1,0:T(8,128)S(1)} %get-tuple-element.200), channel_id=1, source_target_pairs={{1,0},{2,1},{3,2},{4,3},{5,4},{6,5},{7,6},{8,7},{9,8},{10,9},{11,1... | collective-permute-start | bytes 24584 | tf_op jit(solution)/shard_map/ppermute | solution.py:13
  431.3 7.7 %collective-permute-start.45 = (f32[2,1,16,128]{3,2,1,0:T(8,128)S(1)}, f32[2,1,16,128]{3,2,1,0:T(8,128)S(1)}, u32[]{:S(2)}, u32[]{:S(2)}) collective-permute-start(f32[2,1,16,128]{3,2,1,0:T(8,128)S(1)} %pad_maximum_fusion.23), channel_id=1, source_target_pairs={{0,1},{1,2},{2,3},{3,4},{4,5},{5,6},{6,7},{7,8},{8,9},{9,10},{10,1... | collective-permute-start | bytes 49160 | tf_op jit(solution)/shard_map/ppermute | solution.py:13
  439.2 5.9 %collective-permute-start.46 = (f32[1,16,128]{2,1,0:T(8,128)S(1)}, f32[1,16,128]{2,1,0:T(8,128)S(1)}, u32[]{:S(2)}, u32[]{:S(2)}) collective-permute-start(f32[1,16,128]{2,1,0:T(8,128)S(1)} %get-tuple-element.271), channel_id=1, source_target_pairs={{1,0},{2,1},{3,2},{4,3},{5,4},{6,5},{7,6},{8,7},{9,8},{10,9},{11,1... | collective-permute-start | bytes 24584 | tf_op jit(solution)/shard_map/ppermute | solution.py:13
  441.2 7.7 %collective-permute-start.47 = (f32[2,1,16,128]{3,2,1,0:T(8,128)S(1)}, f32[2,1,16,128]{3,2,1,0:T(8,128)S(1)}, u32[]{:S(2)}, u32[]{:S(2)}) collective-permute-start(f32[2,1,16,128]{3,2,1,0:T(8,128)S(1)} %pad_maximum_fusion.24), channel_id=1, source_target_pairs={{0,1},{1,2},{2,3},{3,4},{4,5},{5,6},{6,7},{7,8},{8,9},{9,10},{10,1... | collective-permute-start | bytes 49160 | tf_op jit(solution)/shard_map/ppermute | solution.py:13
  449.1 5.9 %collective-permute-start.48 = (f32[1,16,128]{2,1,0:T(8,128)S(1)}, f32[1,16,128]{2,1,0:T(8,128)S(1)}, u32[]{:S(2)}, u32[]{:S(2)}) collective-permute-start(f32[1,16,128]{2,1,0:T(8,128)S(1)} %get-tuple-element.268), channel_id=1, source_target_pairs={{1,0},{2,1},{3,2},{4,3},{5,4},{6,5},{7,6},{8,7},{9,8},{10,9},{11,1... | collective-permute-start | bytes 24584 | tf_op jit(solution)/shard_map/ppermute | solution.py:13
  451.1 7.7 %collective-permute-start.49 = (f32[2,1,16,128]{3,2,1,0:T(8,128)S(1)}, f32[2,1,16,128]{3,2,1,0:T(8,128)S(1)}, u32[]{:S(2)}, u32[]{:S(2)}) collective-permute-start(f32[2,1,16,128]{3,2,1,0:T(8,128)S(1)} %pad_maximum_fusion.25), channel_id=1, source_target_pairs={{0,1},{1,2},{2,3},{3,4},{4,5},{5,6},{6,7},{7,8},{8,9},{9,10},{10,1... | collective-permute-start | bytes 49160 | tf_op jit(solution)/shard_map/ppermute | solution.py:13
  (15 other events, 38.0 us)
where the time goes:
time: 469 us; the launch traced here: 460 us
  waiting for transfers between devices  175 us (37%)
  starting transfers between devices  168 us (36%)
  matrix products  51 us (11%)
  other arithmetic  38.7 us (8%)
  local copies, waits for them, and re-layouts  24.2 us (5%)
    ppermute x43, waiting for transfers between devices, from_behind(): return lax.ppermute(value, axis, pairs)  132 us
    ppermute x43, starting transfers between devices, from_behind(): return lax.ppermute(value, axis, pairs)  126 us
    all_to_all x6, starting transfers between devices, sent_to_all(): lax.all_to_all(jnp.broadcast_to(value[None], (size, *value.shape)), axis,...  42.1 us
    all_to_all x6, waiting for transfers between devices, sent_to_all(): lax.all_to_all(jnp.broadcast_to(value[None], (size, *value.shape)), axis,...  25 us
    dot_general x4, matrix products, candidate(): jnp.dot(weights, corrections, precision=exact_mode)  24.1 us
    ppermute x7, waiting for transfers between devices, from_behind_2(): return lax.ppermute(value, axis, pairs)  18.6 us
    dot_general x4, matrix products, candidate(): jnp.dot(flat_basis, left_value.reshape(-1), precision=exact_mode)  13.4 us
  transfers between devices with their start and end apart: 56, of which 33 were waited for; matrix products, arithmetic and copies ran while one was open for 14% of the time, Pallas kernels for 0%

commit v1 on v0

v1 whole, which is shorter than its diff:
```python
import functools

import jax
import jax.numpy as jnp
from jax import lax
from jax.experimental import pallas as pl
from jax.experimental.pallas import tpu as pltpu
from jax.sharding import PartitionSpec as P

DT = 0.045
MESH = pl.DeviceIdType.MESH
F32 = jnp.float32

R1, R2, R3, Y1, Y2, Y3, Y4, X2, X3, X4, GAP, LAST = range(12)
ROUNDS = 12

DEEP = ((0, 5), (0, 5), (1, 5), (0, 3))
THREE = ((0, 5), (0, 5), (2, 4), (1, 2))
TWO = ((1, 5), (0, 3))
ONE = ((2, 4), (1, 2))
OFFSETS = (1, -1, 2, -2)


def kernel(
    n_tm,
    n_space,
    rank,
    speed_hbm,
    forcing_hbm,
    guess_hbm,
    basis_hbm,
    states_ref,
    coords_ref,
    b_ref,
    bt_ref,
    bm_ref,
    guess_ref,
    speed_ref,
    force_ref,
    speed_halo,
    force_halo,
    c2_ref,
    msg_ref,
    halo_ref,
    own_ref,
    yown_ref,
    zout_ref,
    zin_ref,
    rel_ref,
    res_ref,
    x_ref,
    gap_ref,
    fin_ref,
    ar_ref,
    gram_ref,
    inv_ref,
    part_ref,
    w_ref,
    local_sem,
    send_sem,
    recv_sem,
    zsend_sem,
    zrecv_sem,
    start_send,
    start_recv,
    arsend_sem,
    arrecv_sem,
    gsend_sem,
    grecv_sem,
):
    t = lax.axis_index("tm")
    s = lax.axis_index("space")

    def at_t(d):
        return lax.rem(t + (d + n_tm), n_tm)

    def at_s(d):
        return lax.rem(s + (d + n_space), n_space)

    loads = [
        pltpu.make_async_copy(guess_hbm.at[0], guess_ref, local_sem.at[0]),
        pltpu.make_async_copy(speed_hbm, speed_ref, local_sem.at[1]),
        pltpu.make_async_copy(forcing_hbm, force_ref, local_sem.at[2]),
        pltpu.make_async_copy(basis_hbm.at[0], b_ref, local_sem.at[3]),
    ]
    for load in loads:
        load.start()

    def start_row(m, carry):
        c = m // 32
        z = lax.rem(m // 16, 2)
        x = lax.rem(m, 16)
        pltpu.make_async_copy(
            basis_hbm.at[0, :, c, z, x, :], bt_ref.at[c, z, x], local_sem.at[4]
        ).start()
        return carry

    barrier = pltpu.get_barrier_semaphore()
    peers = [(dt, ds) for dt in (1, -1) for ds in (-2, -1, 0, 1, 2)]
    peers += [(4, ds) for ds in (-1, 0, 1)]
    peers += [(0, ds) for ds in range(1, n_space)]
    for dt, ds in peers:
        pl.semaphore_signal(
            barrier, inc=1, device_id=(at_t(dt), at_s(ds)), device_id_type=MESH
        )
    lax.fori_loop(0, 128, start_row, 0)
    pl.semaphore_wait(barrier, len(peers))

    sent = []

    def send(src, dst, ssem, rsem, dt, ds):
        copy = pltpu.make_async_remote_copy(
            src_ref=src,
            dst_ref=dst,
            send_sem=ssem,
            recv_sem=rsem,
            device_id=(at_t(dt), at_s(ds)),
            device_id_type=MESH,
        )
        copy.start()
        sent.append(copy)
        return copy

    plane = guess_ref.shape[2:]
    ix = lax.broadcasted_iota(jnp.int32, plane, 0)
    iy = lax.broadcasted_iota(jnp.int32, plane, 1)
    nx, ny = plane
    zero = jnp.zeros(plane, F32)
    x_low, x_high = ix == 0, ix == nx - 1
    y_low, y_high = iy == 0, iy == ny - 1
    weight = 5.0 - x_low.astype(F32) - y_low.astype(F32)

    def x_ahead(v):
        return jnp.where(x_high, zero, pltpu.roll(v, nx - 1, 0))

    def x_behind(v):
        return jnp.where(x_low, zero, pltpu.roll(v, 1, 0))

    def y_ahead(v):
        return jnp.where(y_high, zero, pltpu.roll(v, ny - 1, 1))

    def y_behind(v):
        return jnp.where(y_low, zero, pltpu.roll(v, 1, 1))

    def flag(cond):
        return jnp.where(cond, 1.0, 0.0).astype(F32)

    e_dn1, e_dn2 = flag(s >= 1), flag(s >= 2)
    e_up1, e_up2 = flag(s <= n_space - 2), flag(s <= n_space - 3)
    floor = {0: e_dn1, -2: e_dn2}

    def lap(p, j):
        below = p[j - 1] - p[j]
        if j in floor:
            below = below * floor[j]
        return (
            (x_ahead(p[j]) + x_behind(p[j]))
            + (y_ahead(p[j]) + y_behind(p[j]))
            + (p[j + 1] - weight * p[j])
            + below
        )

    def c2(j):
        return c2_ref[j + 3]

    def force(n, j):
        if j in (0, 1):
            return force_ref[n, j]
        if j in (-1, -2):
            return force_halo[0, n, j + 2] * e_dn1
        if j in (2, 3):
            return force_halo[1, n, j - 2] * e_up1
        if j == -3:
            return force_halo[2, 0, 1] * e_dn2
        return force_halo[3, 0, 0] * e_up2

    def steps(p, d, h, count, forced=False):
        values, first = [p], None
        for n in range(count):
            depth = count - 1 - n
            planes = range(-depth, 2 + depth)
            laps = {j: lap(p, j) for j in planes}
            if first is None:
                first = laps
            d = {j: d[j] - h * laps[j] for j in planes}
            p = {j: p[j] - (h * c2(j)) * d[j] for j in planes}
            if forced:
                p = {j: p[j] + force(n, j) for j in planes}
            values.append(p)
        return values, first

    def grad(p, j):
        return (x_ahead(p[j]) - p[j], y_ahead(p[j]) - p[j], p[j + 1] - p[j])

    def divergence(state):
        both = []
        for z in range(2):
            both.append(
                (state[1][z] - x_behind(state[1][z]))
                + (state[2][z] - y_behind(state[2][z]))
            )
        return both[0] + state[3][0], both[1] + (state[3][1] - state[3][0])

    def load_state(ref):
        return [[ref[c, z] for z in range(2)] for c in range(4)]

    def store_state(ref, state):
        for c in range(4):
            for z in range(2):
                ref[c, z] = state[c][z]

    def combine(fn, *states):
        return [[fn(*[u[c][z] for u in states]) for z in range(2)] for c in range(4)]

    def write_msg(ref, state, deep=True):
        if deep:
            low, high = divergence(state)
            ref[0] = low
            ref[4] = high
        ref[1] = state[0][0]
        ref[2] = state[0][1]
        ref[3] = state[3][1]

    def unpack(halo, own_p, own_d, own_vz, depth):
        p = {0: own_p[0], 1: own_p[1]}
        vz_below = halo[0, 3] * e_dn1
        p[-1] = halo[0, 2] * e_dn1
        p[2] = halo[1, 1] * e_up1
        d = {0: own_d[0] - vz_below, 1: own_d[1]}
        if depth >= 2:
            p[-2] = halo[0, 1] * e_dn1
            p[3] = halo[1, 2] * e_up1
            d[-1] = halo[0, 4]
            d[2] = halo[1, 0] - own_vz
        if depth >= 3:
            p[-3] = halo[2, 2] * e_dn2
            p[4] = halo[3, 1] * e_up2
            d[-2] = halo[0, 0] - halo[2, 3] * e_dn2
            d[3] = halo[1, 4]
        if depth >= 4:
            p[-4] = halo[2, 1] * e_dn2
            p[5] = halo[3, 2] * e_up2
            d[-3] = halo[2, 4]
            d[4] = halo[3, 0] - halo[1, 3]
        return p, d

    def send_halo(i, slices, dt):
        for k, (low, high) in enumerate(slices):
            part = pl.ds(low, high - low)
            send(
                msg_ref.at[i, part],
                halo_ref.at[i, k, part],
                send_sem.at[i, k],
                recv_sem.at[i, k],
                dt,
                OFFSETS[k],
            )

    def wait_halo(i, slices, dt):
        for k, (low, high) in enumerate(slices):
            part = pl.ds(low, high - low)
            pltpu.make_async_remote_copy(
                src_ref=msg_ref.at[i, part],
                dst_ref=halo_ref.at[i, k, part],
                send_sem=send_sem.at[i, k],
                recv_sem=recv_sem.at[i, k],
                device_id=(at_t(dt), at_s(OFFSETS[k])),
                device_id_type=MESH,
            ).wait_recv()

    def send_own(i, src, dst, dt):
        return send(src, dst, send_sem.at[i, 4], recv_sem.at[i, 4], dt, 0)

    def send_state(i, ref, dt):
        return send_own(i, ref, own_ref.at[i], dt)

    def halo_of(i):
        return halo_ref.at[i]

    rows = lax.broadcasted_iota(jnp.int32, (rank, 128), 0)
    lanes = lax.broadcasted_iota(jnp.int32, (rank, 128), 1)
    diagonal = rows == lanes

    def to_row(column):
        spread = jnp.where(diagonal, jnp.broadcast_to(column, (rank, 128)), 0.0)
        return jnp.sum(spread, axis=0, keepdims=True)

    def share_products(i, state_ref):
        def group(g, carry):
            out = []
            for k in range(8):
                total = jnp.zeros((8, 128), F32)
                for c in range(4):
                    for z in range(2):
                        for half in range(nx // 8):
                            part = slice(half * 8, half * 8 + 8)
                            total = total + (
                                b_ref[g * 8 + k, c, z, part, :] * state_ref[c, z, part, :]
                            )
                out.append(jnp.sum(total, axis=0, keepdims=True))
            part_ref[pl.ds(pl.multiple_of(g * 8, 8), 8), :] = jnp.concatenate(out, axis=0)
            return carry

        lax.fori_loop(0, rank // 8, group, 0)
        ar_ref[i, s] = to_row(jnp.sum(part_ref[...], axis=1, keepdims=True))
        for j in range(1, n_space):
            send(
                ar_ref.at[i, s],
                ar_ref.at[i, s],
                arsend_sem.at[i, j],
                arrecv_sem.at[i, j],
                0,
                j,
            )

    def solved(i):
        for j in range(1, n_space):
            pltpu.make_async_remote_copy(
                src_ref=ar_ref.at[i, s],
                dst_ref=ar_ref.at[i, at_s(-j)],
                send_sem=arsend_sem.at[i, j],
                recv_sem=arrecv_sem.at[i, j],
                device_id=(t, at_s(j)),
                device_id_type=MESH,
            ).wait_recv()
        total = ar_ref[i, 0]
        for j in range(1, n_space):
            total = total + ar_ref[i, j]
        moved = pltpu.roll(jnp.broadcast_to(total, (8, 128)), rank, 1)[0:1]
        product = jnp.where(lanes >= rank, inv_ref[...] * moved, 0.0)
        return jnp.sum(product, axis=1, keepdims=True)

    def combine_columns(i, weights):
        w_ref[...] = jnp.broadcast_to(weights, (rank, 128))

        def group(g, acc):
            for k in range(4):
                r = g * 4 + k
                w = jnp.broadcast_to(w_ref[pl.ds(r, 1), :], plane)
                acc = tuple(acc[m] + w * bm_ref[r, m] for m in range(5))
            return acc

        acc = lax.fori_loop(0, rank // 4, group, (zero,) * 5)
        for m in range(5):
            msg_ref[i, m] = acc[m]

    def eliminate(low, high):
        def step(k, carry):
            m = inv_ref[...]
            row = inv_ref[pl.ds(k, 1), :]
            col = jnp.sum(jnp.where(lanes == k, m, 0.0), axis=1, keepdims=True)
            pivot = jnp.sum(jnp.where(lanes[0:1] == k, row, 0.0), axis=1, keepdims=True)
            row = row / pivot
            inv_ref[...] = jnp.where(rows == k, row, m - col * row)
            return carry

        lax.fori_loop(low, high, step, 0)

    loads[0].wait()
    write_msg(msg_ref.at[R1], load_state(guess_ref))
    send_halo(R1, DEEP, 1)
    send_state(R1, guess_ref, 1)
    loads[1].wait()
    loads[2].wait()
    edge = (None, None, pl.ds(1, 1), pl.ds(0, 1))
    starts = []
    for k in range(4):
        if edge[k] is None:
            pair = [
                (speed_ref, speed_halo.at[k]),
                (force_ref.at[pl.ds(0, 3)], force_halo.at[k]),
            ]
        else:
            pair = [
                (speed_ref.at[edge[k]], speed_halo.at[k, edge[k]]),
                (
                    force_ref.at[pl.ds(0, 1), edge[k]],
                    force_halo.at[k, pl.ds(0, 1), edge[k]],
                ),
            ]
        for m, (src, dst) in enumerate(pair):
            starts.append(
                send(src, dst, start_send.at[k, m], start_recv.at[k, m], 0, OFFSETS[k])
            )

    loads[3].wait()

    def column_msg(r, carry):
        state = [[b_ref[r, c, z] for z in range(2)] for c in range(4)]
        write_msg(bm_ref.at[r], state)
        return carry

    lax.fori_loop(0, rank, column_msg, 0)
    pltpu.make_async_copy(bt_ref, bt_ref, local_sem.at[4]).wait()

    def gram_part(i, acc):
        c = i // 4
        z = lax.rem(i // 2, 2)
        x = lax.rem(i, 2) * 8
        flat = jnp.concatenate([bt_ref[c, z, x + k] for k in range(8)], axis=1)
        return acc + lax.dot_general(
            flat,
            flat,
            (((1,), (1,)), ((), ())),
            precision=lax.Precision.HIGHEST,
            preferred_element_type=F32,
        )

    gram = lax.fori_loop(0, 16, gram_part, jnp.zeros((rank, rank), F32))
    half = rank // 2
    gram_ref[s] = jnp.concatenate([gram[:half], gram[half:]], axis=1)
    for j in range(1, n_space):
        send(gram_ref.at[s], gram_ref.at[s], gsend_sem.at[j], grecv_sem.at[j], 0, j)

    for copy in starts:
        copy.wait_recv()
    for j, value, on in (
        (0, speed_ref[0], None),
        (1, speed_ref[1], None),
        (-1, speed_halo[0, 1], e_dn1),
        (-2, speed_halo[0, 0], e_dn1),
        (2, speed_halo[1, 0], e_up1),
        (3, speed_halo[1, 1], e_up1),
        (-3, speed_halo[2, 1], e_dn2),
        (4, speed_halo[3, 0], e_up2),
    ):
        squared = value * value
        c2_ref[j + 3] = squared if on is None else squared * on

    def four_forced(i):
        wait_halo(i, DEEP, 1)
        state = load_state(own_ref.at[i])
        low, high = divergence(state)
        p, d = unpack(halo_of(i), state[0], (low, high), state[3][1], 4)
        values, _ = steps(p, d, DT, 4, forced=True)
        total = {
            j: (values[0][j] + values[1][j]) + (values[2][j] + values[3][j])
            for j in range(0, 3)
        }
        out = [[values[4][0], values[4][1]], [None] * 2, [None] * 2, [None] * 2]
        for z in range(2):
            for c, slope in enumerate(grad(total, z)):
                out[c + 1][z] = state[c + 1][z] - DT * slope
        return out

    def wait_state(i, dt):
        pltpu.make_async_remote_copy(
            src_ref=own_ref.at[i],
            dst_ref=own_ref.at[i],
            send_sem=send_sem.at[i, 4],
            recv_sem=recv_sem.at[i, 4],
            device_id=(at_t(dt), s),
            device_id_type=MESH,
        ).wait_recv()

    wait_state(R1, 1)
    relaxed = four_forced(R1)
    store_state(rel_ref, relaxed)
    write_msg(msg_ref.at[R2], relaxed)
    send_halo(R2, DEEP, 1)
    send_state(R2, rel_ref, 1)

    for j in range(1, n_space):
        pltpu.make_async_remote_copy(
            src_ref=gram_ref.at[s],
            dst_ref=gram_ref.at[at_s(-j)],
            send_sem=gsend_sem.at[j],
            recv_sem=grecv_sem.at[j],
            device_id=(t, at_s(j)),
            device_id_type=MESH,
        ).wait_recv()
    whole = gram_ref[0]
    for j in range(1, n_space):
        whole = whole + gram_ref[j]
    unit = (lanes == rows + rank).astype(F32)
    left = lanes[:half] < rank
    inv_ref[0:half, :] = jnp.where(left, whole, unit[:half])
    inv_ref[half:rank, :] = jnp.where(left, pltpu.roll(whole, 128 - rank, 1), unit[half:])
    eliminate(0, 24)

    wait_state(R2, 1)
    residue = combine(lambda a, b: a - b, four_forced(R2), load_state(rel_ref))
    store_state(res_ref, residue)
    write_msg(msg_ref.at[R3], residue, deep=False)
    send_state(R3, res_ref, 1)
    send_halo(R3, ONE, 1)
    eliminate(24, 40)

    def coarse(state, halo):
        p, d = unpack(halo, state[0], divergence(state), None, 1)
        values, _ = steps(p, d, 4 * DT, 1)
        out = [[values[1][0], values[1][1]], [None] * 2, [None] * 2, [None] * 2]
        for z in range(2):
            for c, slope in enumerate(grad(p, z)):
                out[c + 1][z] = state[c + 1][z] - (4 * DT) * slope
        return out

    def correction(halo, own):
        p, d = unpack(halo, (own[1], own[2]), (own[0], own[4]), own[3], 4)
        values, first = steps(p, d, DT, 4)
        out = [[None] * 2 for _ in range(4)]
        for z in range(2):
            slow = p[z] - (4 * DT * c2(z)) * (d[z] - (4 * DT) * first[z])
            out[0][z] = values[4][z] - slow
        total = {
            j: (values[1][j] - p[j]) + (values[2][j] - p[j]) + (values[3][j] - p[j])
            for j in range(0, 3)
        }
        for z in range(2):
            for c, slope in enumerate(grad(total, z)):
                out[c + 1][z] = -DT * slope
        return out

    def add(a, b):
        return a + b

    def candidate(n, i_y, i_x, x_state_ref, last):
        share_products(n, x_state_ref)
        wait_halo(i_x, ONE, 1 if i_x == R3 else 0)
        z = combine(add, coarse(load_state(x_state_ref), halo_of(i_x)), load_state(res_ref))
        store_state(zout_ref.at[n], z)
        if not last:
            send(zout_ref.at[n], zin_ref.at[n], zsend_sem.at[n], zrecv_sem.at[n], 1, 0)
        if n == 0:
            eliminate(40, rank)
        combine_columns(i_y, solved(n))
        dt = 0 if last else 1
        send_halo(i_y, DEEP, dt)
        if last:
            wait_halo(i_y, DEEP, dt)
            return combine(
                add,
                load_state(zout_ref.at[n]),
                correction(halo_of(i_y), msg_ref.at[i_y]),
            )
        own = send_own(i_y, msg_ref.at[i_y], yown_ref.at[n], dt)
        pltpu.make_async_remote_copy(
            src_ref=zout_ref.at[n],
            dst_ref=zin_ref.at[n],
            send_sem=zsend_sem.at[n],
            recv_sem=zrecv_sem.at[n],
            device_id=(at_t(1), s),
            device_id_type=MESH,
        ).wait_recv()
        own.wait_recv()
        wait_halo(i_y, DEEP, dt)
        return combine(
            add, load_state(zin_ref.at[n]), correction(halo_of(i_y), yown_ref.at[n])
        )

    def announce(i, ref, state):
        store_state(ref, state)
        write_msg(msg_ref.at[i], state, deep=False)
        send_halo(i, ONE, 0)

    wait_state(R3, 1)
    announce(X2, x_ref.at[0], candidate(0, Y1, R3, own_ref.at[R3], False))
    announce(X3, x_ref.at[1], candidate(1, Y2, X2, x_ref.at[0], False))
    third = candidate(2, Y3, X3, x_ref.at[1], False)
    store_state(x_ref.at[2], third)

    gap = combine(lambda a, b: a - b, third, load_state(x_ref.at[1]))
    store_state(gap_ref, gap)
    write_msg(msg_ref.at[GAP], gap)
    send_halo(GAP, TWO, 4)
    send_state(GAP, gap_ref, 4)
    wait_halo(GAP, TWO, 4)
    wait_state(GAP, 4)
    state = load_state(own_ref.at[GAP])
    p, d = unpack(halo_of(GAP), state[0], divergence(state), state[3][1], 2)
    values, _ = steps(p, d, 8 * DT, 2)
    total = {j: values[0][j] + values[1][j] for j in range(0, 3)}
    behind = [[values[2][0], values[2][1]], [None] * 2, [None] * 2, [None] * 2]
    for z in range(2):
        for c, slope in enumerate(grad(total, z)):
            behind[c + 1][z] = state[c + 1][z] - (8 * DT) * slope
    late = flag(lax.rem(t + (n_tm - 1), n_tm) >= 4)
    announce(
        X4,
        x_ref.at[3],
        combine(lambda a, b: a + late * b, load_state(x_ref.at[2]), behind),
    )
    levels = candidate(3, Y4, X4, x_ref.at[3], True)

    final = combine(add, load_state(rel_ref), levels)
    store_state(fin_ref, final)
    write_msg(msg_ref.at[LAST], final)
    send_halo(LAST, THREE, 1)
    send_state(LAST, fin_ref, 1)
    share_products(4, fin_ref)
    store_state(states_ref.at[3], final)
    wait_state(LAST, 1)
    wait_halo(LAST, THREE, 1)
    state = load_state(own_ref.at[LAST])
    p, d = unpack(halo_of(LAST), state[0], divergence(state), state[3][1], 3)
    values, _ = steps(p, d, DT, 3, forced=True)
    for n in range(3):
        for z in range(2):
            state[0][z] = values[n + 1][z]
            for c, slope in enumerate(grad(values[n], z)):
                state[c + 1][z] = state[c + 1][z] - DT * slope
        store_state(states_ref.at[n], state)
    coords_ref[...] = to_row(solved(4))[:, :rank]

    for copy in sent:
        copy.wait_send()


def body(n_tm, n_space, speed, forcing, guess, basis):
    rank = basis.shape[1]
    plane = speed.shape[1:]
    vmem = functools.partial(pltpu.VMEM, dtype=F32)
    dma = pltpu.SemaphoreType.DMA
    state = (4, 2, *plane)
    msg = (5, *plane)
    scratch = [
        vmem((rank, *state)),
        vmem((4, 2, plane[0], rank, plane[1])),
        vmem((rank, *msg)),
        vmem(state),
        vmem((2, *plane)),
        vmem((4, 2, *plane)),
        vmem((4, 2, *plane)),
        vmem((4, 3, 2, *plane)),
        vmem((8, *plane)),
        vmem((ROUNDS, *msg)),
        vmem((ROUNDS, 4, *msg)),
        vmem((ROUNDS, *state)),
        vmem((3, *msg)),
        vmem((4, *state)),
        vmem((3, *state)),
        vmem(state),
        vmem(state),
        vmem((4, *state)),
        vmem(state),
        vmem(state),
        vmem((5, n_space, 1, 128)),
        vmem((n_space, rank // 2, 128)),
        vmem((rank, 128)),
        vmem((rank, 128)),
        vmem((rank, 128)),
        dma((5,)),
        dma((ROUNDS, 5)),
        dma((ROUNDS, 5)),
        dma((3,)),
        dma((3,)),
        dma((4, 2)),
        dma((4, 2)),
        dma((5, n_space)),
        dma((5, n_space)),
        dma((n_space,)),
        dma((n_space,)),
    ]
    return pl.pallas_call(
        functools.partial(kernel, n_tm, n_space, rank),
        out_shape=(
            jax.ShapeDtypeStruct((4, *state), F32),
            jax.ShapeDtypeStruct((1, rank), F32),
        ),
        in_specs=[pl.BlockSpec(memory_space=pl.ANY)] * 4,
        out_specs=(
            pl.BlockSpec(memory_space=pltpu.VMEM),
            pl.BlockSpec(memory_space=pltpu.VMEM),
        ),
        scratch_shapes=scratch,
        compiler_params=pltpu.CompilerParams(collective_id=0, has_side_effects=True),
    )(speed, forcing, guess, basis)


def solution(mesh):
    placed = (
        P("space", None, None),
        P("tm", "space", None, None),
        P("tm", None, "space", None, None),
        P("tm", None, None, "space", None, None),
    )
    return jax.shard_map(
        functools.partial(body, mesh.shape["tm"], mesh.shape["space"]),
        mesh=mesh,
        in_specs=placed,
        out_specs=(P("tm", None, "space", None, None), P("tm", None)),
        check_vma=False,
    )
```

time: 469 us -> 95.9 us (0.20)
  the two profiles are of different devices: /device:TPU:38 before, /device:TPU:0 now
where the time goes in v1:
time: 95.9 us; the launch traced here: 94.9 us
  Pallas kernels  91.5 us (95%)
  local copies, waits for them, and re-layouts  2.8 us (3%)
    pallas_call x1, Pallas kernels, body(): pl.pallas_call(functools.partial(kernel, n_tm, n_space, rank), out_shape=...  91.5 us
    unnamed x2, local copies, waits for them, and re-layouts  2.8 us

profile of v1, /device:TPU:0, one launch (start us, length us, event | category | flops | bytes accessed | tf_op | source)
XLA Modules:
  0.0 94.9 jit_solution(9758018173384425399)
XLA Ops:
  0.6 91.5 %shard_map.59 = (f32[4,4,2,16,128]{4,3,2,1,0:T(8,128)}, f32[1,64]{1,0:T(1,128)}) custom-call(f32[2,16,128]{2,1,0:T(8,128)} %speed_hbm.1, f32[4,2,16,128]{3,2,1,0:T(8,128)} %forcing_hbm.1, f32[1,4,2,16,128]{4,3,2,1,0:T(8,128)} %guess_hbm.1, f32[1,64,4,2,16,128]{5,4,3,2,1,0:T(8,128)} %basis_hbm.1), custom_call_target="tpu_custom_call" | custom-call | tf_op jit(solution)/shard_map/pallas_call | solution.py:654
  92.1 1.7 %copy.8 = f32[4,4,2,16,128]{4,3,2,1,0:T(8,128)} copy(f32[4,4,2,16,128]{4,3,2,1,0:T(8,128)} %get-tuple-element.4) | data formatting | bytes 524288
  93.8 1.1 %copy.9 = f32[1,64]{1,0:T(1,128)} copy(f32[1,64]{1,0:T(1,128)} %get-tuple-element.5) | data formatting | bytes 512

commit v2 on v1

--- a/solution.py
+++ b/solution.py
@@ -1,4 +1,5 @@
 import functools
+import math
 
 import jax
 import jax.numpy as jnp
@@ -58,16 +59,13 @@
     w_ref,
     local_sem,
     send_sem,
+    gap_sem,
     recv_sem,
-    zsend_sem,
-    zrecv_sem,
-    start_send,
-    start_recv,
-    arsend_sem,
-    arrecv_sem,
-    gsend_sem,
-    grecv_sem,
+    ar_send_sem,
+    ar_sem,
+    gram_sem,
 ):
+    plane = guess_ref.shape[2:]
     t = lax.axis_index("tm")
     s = lax.axis_index("space")
 
@@ -86,42 +84,48 @@
     for load in loads:
         load.start()
 
-    def start_row(m, carry):
-        c = m // 32
-        z = lax.rem(m // 16, 2)
-        x = lax.rem(m, 16)
-        pltpu.make_async_copy(
-            basis_hbm.at[0, :, c, z, x, :], bt_ref.at[c, z, x], local_sem.at[4]
-        ).start()
+    def start_rows(m, carry):
+        c = m // 2
+        z = lax.rem(m, 2)
+        for x in range(plane[0]):
+            pltpu.make_async_copy(
+                basis_hbm.at[0, :, c, z, x, :], bt_ref.at[c, z, x], local_sem.at[4]
+            ).start()
         return carry
 
     barrier = pltpu.get_barrier_semaphore()
     peers = [(dt, ds) for dt in (1, -1) for ds in (-2, -1, 0, 1, 2)]
     peers += [(4, ds) for ds in (-1, 0, 1)]
     peers += [(0, ds) for ds in range(1, n_space)]
-    for dt, ds in peers:
-        pl.semaphore_signal(
-            barrier, inc=1, device_id=(at_t(dt), at_s(ds)), device_id_type=MESH
-        )
-    lax.fori_loop(0, 128, start_row, 0)
-    pl.semaphore_wait(barrier, len(peers))
+    with jax.named_scope("signals"):
+        for dt, ds in peers:
+            pl.semaphore_signal(
+                barrier, inc=1, device_id=(at_t(dt), at_s(ds)), device_id_type=MESH
+            )
+    with jax.named_scope("rows"):
+        lax.fori_loop(0, 8, start_rows, 0)
 
     sent = []
 
-    def send(src, dst, ssem, rsem, dt, ds):
-        copy = pltpu.make_async_remote_copy(
+    def words(ref):
+        return math.prod(ref.shape)
+
+    def send(src, dst, rsem, dt, ds, ssem=None):
+        pltpu.make_async_remote_copy(
             src_ref=src,
             dst_ref=dst,
-            send_sem=ssem,
+            send_sem=send_sem.at[0] if ssem is None else ssem,
             recv_sem=rsem,
             device_id=(at_t(dt), at_s(ds)),
             device_id_type=MESH,
-        )
-        copy.start()
-        sent.append(copy)
-        return copy
-
-    plane = guess_ref.shape[2:]
+        ).start()
+        if ssem is None:
+            sent.append(words(src))
+
+    def wait_planes(sem, planes):
+        part = bm_ref.reshape(rank * 5, *plane).at[pl.ds(0, planes)]
+        pltpu.make_async_copy(part, part, sem).wait()
+
     ix = lax.broadcasted_iota(jnp.int32, plane, 0)
     iy = lax.broadcasted_iota(jnp.int32, plane, 1)
     nx, ny = plane
@@ -244,35 +248,31 @@
             d[4] = halo[3, 0] - halo[1, 3]
         return p, d
 
-    def send_halo(i, slices, dt):
-        for k, (low, high) in enumerate(slices):
+    def send_halo(i, slices, dt, ssem=None):
+        for k in reversed(range(len(slices))):
+            low, high = slices[k]
             part = pl.ds(low, high - low)
             send(
                 msg_ref.at[i, part],
                 halo_ref.at[i, k, part],
-                send_sem.at[i, k],
-                recv_sem.at[i, k],
+                recv_sem.at[i],
                 dt,
                 OFFSETS[k],
+                ssem,
             )
 
-    def wait_halo(i, slices, dt):
-        for k, (low, high) in enumerate(slices):
-            part = pl.ds(low, high - low)
-            pltpu.make_async_remote_copy(
-                src_ref=msg_ref.at[i, part],
-                dst_ref=halo_ref.at[i, k, part],
-                send_sem=send_sem.at[i, k],
-                recv_sem=recv_sem.at[i, k],
-                device_id=(at_t(dt), at_s(OFFSETS[k])),
-                device_id_type=MESH,
-            ).wait_recv()
-
-    def send_own(i, src, dst, dt):
-        return send(src, dst, send_sem.at[i, 4], recv_sem.at[i, 4], dt, 0)
-
-    def send_state(i, ref, dt):
-        return send_own(i, ref, own_ref.at[i], dt)
+    def planes_of(slices):
+        return sum(high - low for low, high in slices)
+
+    def send_own(i, src, dst, dt, ssem=None):
+        send(src, dst, recv_sem.at[i], dt, 0, ssem)
+
+    def send_state(i, ref, dt, ssem=None):
+        send_own(i, ref, own_ref.at[i], dt, ssem)
+
+    def wait_round(i, slices, more):
+        with jax.named_scope(f"wait_round{i}"):
+            wait_planes(recv_sem.at[i], planes_of(slices) + more)
 
     def halo_of(i):
         return halo_ref.at[i]
@@ -281,6 +281,8 @@
     lanes = lax.broadcasted_iota(jnp.int32, (rank, 128), 1)
     diagonal = rows == lanes
 
+    far_first = sorted(range(1, n_space), key=lambda j: abs(abs(j - n_space // 2) - 2))
+
     def to_row(column):
         spread = jnp.where(diagonal, jnp.broadcast_to(column, (rank, 128)), 0.0)
         return jnp.sum(spread, axis=0, keepdims=True)
@@ -288,41 +290,29 @@
     def share_products(i, state_ref):
         def group(g, carry):
             out = []
-            for k in range(8):
+            for k in range(16):
                 total = jnp.zeros((8, 128), F32)
                 for c in range(4):
                     for z in range(2):
                         for half in range(nx // 8):
                             part = slice(half * 8, half * 8 + 8)
                             total = total + (
-                                b_ref[g * 8 + k, c, z, part, :] * state_ref[c, z, part, :]
+                                b_ref[g * 16 + k, c, z, part, :] * state_ref[c, z, part, :]
                             )
                 out.append(jnp.sum(total, axis=0, keepdims=True))
-            part_ref[pl.ds(pl.multiple_of(g * 8, 8), 8), :] = jnp.concatenate(out, axis=0)
+            part_ref[pl.ds(pl.multiple_of(g * 16, 16), 16), :] = jnp.concatenate(out, axis=0)
             return carry
 
-        lax.fori_loop(0, rank // 8, group, 0)
-        ar_ref[i, s] = to_row(jnp.sum(part_ref[...], axis=1, keepdims=True))
-        for j in range(1, n_space):
-            send(
-                ar_ref.at[i, s],
-                ar_ref.at[i, s],
-                arsend_sem.at[i, j],
-                arrecv_sem.at[i, j],
-                0,
-                j,
-            )
+        with jax.named_scope(f"products{i}"):
+            lax.fori_loop(0, rank // 16, group, 0)
+            ar_ref[i, s] = to_row(jnp.sum(part_ref[...], axis=1, keepdims=True))
+            for j in far_first:
+                send(ar_ref.at[i, s], ar_ref.at[i, s], ar_sem.at[i], 0, j, ar_send_sem.at[i])
 
     def solved(i):
-        for j in range(1, n_space):
-            pltpu.make_async_remote_copy(
-                src_ref=ar_ref.at[i, s],
-                dst_ref=ar_ref.at[i, at_s(-j)],
-                send_sem=arsend_sem.at[i, j],
-                recv_sem=arrecv_sem.at[i, j],
-                device_id=(t, at_s(j)),
-                device_id_type=MESH,
-            ).wait_recv()
+        with jax.named_scope(f"wait_ar{i}"):
+            part = ar_ref.at[i, pl.ds(0, n_space - 1)]
+            pltpu.make_async_copy(part, part, ar_sem.at[i]).wait()
         total = ar_ref[i, 0]
         for j in range(1, n_space):
             total = total + ar_ref[i, j]
@@ -340,9 +330,10 @@
                 acc = tuple(acc[m] + w * bm_ref[r, m] for m in range(5))
             return acc
 
-        acc = lax.fori_loop(0, rank // 4, group, (zero,) * 5)
-        for m in range(5):
-            msg_ref[i, m] = acc[m]
+        with jax.named_scope(f"columns{i}"):
+            acc = lax.fori_loop(0, rank // 4, group, (zero,) * 5)
+            for m in range(5):
+                msg_ref[i, m] = acc[m]
 
     def eliminate(low, high):
         def step(k, carry):
@@ -354,17 +345,63 @@
             inv_ref[...] = jnp.where(rows == k, row, m - col * row)
             return carry
 
-        lax.fori_loop(low, high, step, 0)
-
-    loads[0].wait()
+        with jax.named_scope(f"eliminate{low}"):
+            lax.fori_loop(low, high, step, 0)
+
+    def wait_rows():
+        with jax.named_scope("wait_bt"):
+            pltpu.make_async_copy(bt_ref, bt_ref, local_sem.at[4]).wait()
+
+    def gram_part(i, acc):
+        c = i // 4
+        z = lax.rem(i // 2, 2)
+        x = lax.rem(i, 2) * 8
+        flat = jnp.concatenate([bt_ref[c, z, x + k] for k in range(8)], axis=1)
+        high = flat.astype(jnp.bfloat16)
+        rest = flat - high.astype(F32)
+        middle = rest.astype(jnp.bfloat16)
+        low = (rest - middle.astype(F32)).astype(jnp.bfloat16)
+        stacked = jnp.concatenate([high, middle, low], axis=0)
+        return acc + lax.dot_general(
+            stacked,
+            stacked,
+            (((1,), (1,)), ((), ())),
+            preferred_element_type=F32,
+        )
+
+    def send_gram():
+        with jax.named_scope("gram"):
+            acc = lax.fori_loop(0, 16, gram_part, jnp.zeros((3 * rank, 3 * rank), F32))
+        acc = acc[2 * rank :] + acc[rank : 2 * rank] + acc[:rank]
+        gram = acc[:, 2 * rank :] + acc[:, rank : 2 * rank] + acc[:, :rank]
+        half = rank // 2
+        gram_ref[s] = jnp.concatenate([gram[:half], gram[half:]], axis=1)
+        for j in far_first:
+            send(gram_ref.at[s], gram_ref.at[s], gram_sem.at[0], 0, j)
+
+    with jax.named_scope("wait_basis"):
+        loads[3].wait()
+
+    def column_msg(g, carry):
+        for k in range(8):
+            write_msg(bm_ref.at[g * 8 + k], load_state(b_ref.at[g * 8 + k]))
+        return carry
+
+    with jax.named_scope("column_msg"):
+        lax.fori_loop(0, rank // 8, column_msg, 0)
+    with jax.named_scope("barrier"):
+        pl.semaphore_wait(barrier, len(peers))
+
+    with jax.named_scope("wait_guess"):
+        loads[0].wait()
     write_msg(msg_ref.at[R1], load_state(guess_ref))
     send_halo(R1, DEEP, 1)
     send_state(R1, guess_ref, 1)
-    loads[1].wait()
-    loads[2].wait()
+    with jax.named_scope("wait_load12"):
+        loads[1].wait()
+        loads[2].wait()
     edge = (None, None, pl.ds(1, 1), pl.ds(0, 1))
-    starts = []
-    for k in range(4):
+    for k in (3, 2, 1, 0):
         if edge[k] is None:
             pair = [
                 (speed_ref, speed_halo.at[k]),
@@ -378,42 +415,13 @@
                     force_halo.at[k, pl.ds(0, 1), edge[k]],
                 ),
             ]
-        for m, (src, dst) in enumerate(pair):
-            starts.append(
-                send(src, dst, start_send.at[k, m], start_recv.at[k, m], 0, OFFSETS[k])
-            )
-
-    loads[3].wait()
-
-    def column_msg(r, carry):
-        state = [[b_ref[r, c, z] for z in range(2)] for c in range(4)]
-        write_msg(bm_ref.at[r], state)
-        return carry
-
-    lax.fori_loop(0, rank, column_msg, 0)
-    pltpu.make_async_copy(bt_ref, bt_ref, local_sem.at[4]).wait()
-
-    def gram_part(i, acc):
-        c = i // 4
-        z = lax.rem(i // 2, 2)
-        x = lax.rem(i, 2) * 8
-        flat = jnp.concatenate([bt_ref[c, z, x + k] for k in range(8)], axis=1)
-        return acc + lax.dot_general(
-            flat,
-            flat,
-            (((1,), (1,)), ((), ())),
-            precision=lax.Precision.HIGHEST,
-            preferred_element_type=F32,
-        )
-
-    gram = lax.fori_loop(0, 16, gram_part, jnp.zeros((rank, rank), F32))
-    half = rank // 2
-    gram_ref[s] = jnp.concatenate([gram[:half], gram[half:]], axis=1)
-    for j in range(1, n_space):
-        send(gram_ref.at[s], gram_ref.at[s], gsend_sem.at[j], grecv_sem.at[j], 0, j)
-
-    for copy in starts:
-        copy.wait_recv()
+        for src, dst in pair:
+            send(src, dst, recv_sem.at[R1], 0, OFFSETS[k])
+
+    wait_rows()
+    send_gram()
+
+    wait_round(R1, DEEP, 8 + 6 + 14)
     for j, value, on in (
         (0, speed_ref[0], None),
         (1, speed_ref[1], None),
@@ -428,7 +436,6 @@
         c2_ref[j + 3] = squared if on is None else squared * on
 
     def four_forced(i):
-        wait_halo(i, DEEP, 1)
         state = load_state(own_ref.at[i])
         low, high = divergence(state)
         p, d = unpack(halo_of(i), state[0], (low, high), state[3][1], 4)
@@ -443,48 +450,32 @@
                 out[c + 1][z] = state[c + 1][z] - DT * slope
         return out
 
-    def wait_state(i, dt):
-        pltpu.make_async_remote_copy(
-            src_ref=own_ref.at[i],
-            dst_ref=own_ref.at[i],
-            send_sem=send_sem.at[i, 4],
-            recv_sem=recv_sem.at[i, 4],
-            device_id=(at_t(dt), s),
-            device_id_type=MESH,
-        ).wait_recv()
-
-    wait_state(R1, 1)
     relaxed = four_forced(R1)
     store_state(rel_ref, relaxed)
     write_msg(msg_ref.at[R2], relaxed)
     send_halo(R2, DEEP, 1)
     send_state(R2, rel_ref, 1)
 
-    for j in range(1, n_space):
-        pltpu.make_async_remote_copy(
-            src_ref=gram_ref.at[s],
-            dst_ref=gram_ref.at[at_s(-j)],
-            send_sem=gsend_sem.at[j],
-            recv_sem=grecv_sem.at[j],
-            device_id=(t, at_s(j)),
-            device_id_type=MESH,
-        ).wait_recv()
+    wait_round(R2, DEEP, 8)
+    residue = combine(lambda a, b: a - b, four_forced(R2), load_state(rel_ref))
+    store_state(res_ref, residue)
+    write_msg(msg_ref.at[R3], residue, deep=False)
+    send_state(R3, res_ref, 1)
+    send_halo(R3, ONE, 1)
+
+    with jax.named_scope("wait_gram"):
+        part = gram_ref.at[pl.ds(0, n_space - 1)]
+        pltpu.make_async_copy(part, part, gram_sem.at[0]).wait()
     whole = gram_ref[0]
     for j in range(1, n_space):
         whole = whole + gram_ref[j]
+    half = rank // 2
     unit = (lanes == rows + rank).astype(F32)
     left = lanes[:half] < rank
     inv_ref[0:half, :] = jnp.where(left, whole, unit[:half])
     inv_ref[half:rank, :] = jnp.where(left, pltpu.roll(whole, 128 - rank, 1), unit[half:])
     eliminate(0, 24)
 
-    wait_state(R2, 1)
-    residue = combine(lambda a, b: a - b, four_forced(R2), load_state(rel_ref))
-    store_state(res_ref, residue)
-    write_msg(msg_ref.at[R3], residue, deep=False)
-    send_state(R3, res_ref, 1)
-    send_halo(R3, ONE, 1)
-    eliminate(24, 40)
 
     def coarse(state, halo):
         p, d = unpack(halo, state[0], divergence(state), None, 1)
@@ -516,34 +507,26 @@
 
     def candidate(n, i_y, i_x, x_state_ref, last):
         share_products(n, x_state_ref)
-        wait_halo(i_x, ONE, 1 if i_x == R3 else 0)
+        if i_x != R3:
+            wait_round(i_x, ONE, 0)
         z = combine(add, coarse(load_state(x_state_ref), halo_of(i_x)), load_state(res_ref))
         store_state(zout_ref.at[n], z)
         if not last:
-            send(zout_ref.at[n], zin_ref.at[n], zsend_sem.at[n], zrecv_sem.at[n], 1, 0)
+            send(zout_ref.at[n], zin_ref.at[n], recv_sem.at[i_y], 1, 0)
         if n == 0:
-            eliminate(40, rank)
+            eliminate(24, rank)
         combine_columns(i_y, solved(n))
         dt = 0 if last else 1
         send_halo(i_y, DEEP, dt)
         if last:
-            wait_halo(i_y, DEEP, dt)
+            wait_round(i_y, DEEP, 0)
             return combine(
                 add,
                 load_state(zout_ref.at[n]),
                 correction(halo_of(i_y), msg_ref.at[i_y]),
             )
-        own = send_own(i_y, msg_ref.at[i_y], yown_ref.at[n], dt)
-        pltpu.make_async_remote_copy(
-            src_ref=zout_ref.at[n],
-            dst_ref=zin_ref.at[n],
-            send_sem=zsend_sem.at[n],
-            recv_sem=zrecv_sem.at[n],
-            device_id=(at_t(1), s),
-            device_id_type=MESH,
-        ).wait_recv()
-        own.wait_recv()
-        wait_halo(i_y, DEEP, dt)
+        send_own(i_y, msg_ref.at[i_y], yown_ref.at[n], dt)
+        wait_round(i_y, DEEP, 5 + 8)
         return combine(
             add, load_state(zin_ref.at[n]), correction(halo_of(i_y), yown_ref.at[n])
         )
@@ -553,7 +536,7 @@
         write_msg(msg_ref.at[i], state, deep=False)
         send_halo(i, ONE, 0)
 
-    wait_state(R3, 1)
+    wait_round(R3, ONE, 8)
     announce(X2, x_ref.at[0], candidate(0, Y1, R3, own_ref.at[R3], False))
     announce(X3, x_ref.at[1], candidate(1, Y2, X2, x_ref.at[0], False))
     third = candidate(2, Y3, X3, x_ref.at[1], False)
@@ -562,24 +545,30 @@
     gap = combine(lambda a, b: a - b, third, load_state(x_ref.at[1]))
     store_state(gap_ref, gap)
     write_msg(msg_ref.at[GAP], gap)
-    send_halo(GAP, TWO, 4)
-    send_state(GAP, gap_ref, 4)
-    wait_halo(GAP, TWO, 4)
-    wait_state(GAP, 4)
-    state = load_state(own_ref.at[GAP])
-    p, d = unpack(halo_of(GAP), state[0], divergence(state), state[3][1], 2)
-    values, _ = steps(p, d, 8 * DT, 2)
-    total = {j: values[0][j] + values[1][j] for j in range(0, 3)}
-    behind = [[values[2][0], values[2][1]], [None] * 2, [None] * 2, [None] * 2]
-    for z in range(2):
-        for c, slope in enumerate(grad(total, z)):
-            behind[c + 1][z] = state[c + 1][z] - (8 * DT) * slope
-    late = flag(lax.rem(t + (n_tm - 1), n_tm) >= 4)
-    announce(
-        X4,
-        x_ref.at[3],
-        combine(lambda a, b: a + late * b, load_state(x_ref.at[2]), behind),
-    )
+    store_state(x_ref.at[3], third)
+    early = jnp.logical_and(t >= 1, t <= n_tm - 4)
+    late = jnp.logical_or(t == 0, t >= n_tm - 3)
+
+    @pl.when(early)
+    def _():
+        send_halo(GAP, TWO, 4, gap_sem.at[0])
+        send_state(GAP, gap_ref, 4, gap_sem.at[0])
+
+    @pl.when(late)
+    def _():
+        wait_round(GAP, TWO, 8)
+        state = load_state(own_ref.at[GAP])
+        p, d = unpack(halo_of(GAP), state[0], divergence(state), state[3][1], 2)
+        values, _ = steps(p, d, 8 * DT, 2)
+        total = {j: values[0][j] + values[1][j] for j in range(0, 3)}
+        behind = [[values[2][0], values[2][1]], [None] * 2, [None] * 2, [None] * 2]
+        for z in range(2):
+            for c, slope in enumerate(grad(total, z)):
+                behind[c + 1][z] = state[c + 1][z] - (8 * DT) * slope
+        store_state(x_ref.at[3], combine(add, load_state(x_ref.at[2]), behind))
+
+    write_msg(msg_ref.at[X4], load_state(x_ref.at[3]), deep=False)
+    send_halo(X4, ONE, 0)
     levels = candidate(3, Y4, X4, x_ref.at[3], True)
 
     final = combine(add, load_state(rel_ref), levels)
@@ -589,8 +578,7 @@
     send_state(LAST, fin_ref, 1)
     share_products(4, fin_ref)
     store_state(states_ref.at[3], final)
-    wait_state(LAST, 1)
-    wait_halo(LAST, THREE, 1)
+    wait_round(LAST, THREE, 8)
     state = load_state(own_ref.at[LAST])
     p, d = unpack(halo_of(LAST), state[0], divergence(state), state[3][1], 3)
     values, _ = steps(p, d, DT, 3, forced=True)
@@ -602,8 +590,26 @@
         store_state(states_ref.at[n], state)
     coords_ref[...] = to_row(solved(4))[:, :rank]
 
-    for copy in sent:
-        copy.wait_send()
+    with jax.named_scope("wait_sends"):
+        wait_planes(send_sem.at[0], sum(sent) // math.prod(plane))
+        for i in range(5):
+            part = ar_ref.at[i, pl.ds(0, n_space - 1)]
+            pltpu.make_async_copy(part, part, ar_send_sem.at[i]).wait()
+
+        @pl.when(early)
+        def _():
+            wait_planes(gap_sem.at[0], planes_of(TWO) + 8)
+
+
+def finish(states_ref, coords_ref, states_out, coords_out, sem):
+    copies = [
+        pltpu.make_async_copy(states_ref, states_out, sem.at[0]),
+        pltpu.make_async_copy(coords_ref, coords_out, sem.at[1]),
+    ]
+    for copy in copies:
+        copy.start()
+    for copy in copies:
+        copy.wait()
 
 
 def body(n_tm, n_space, speed, forcing, guess, basis):
@@ -640,22 +646,18 @@
         vmem((rank, 128)),
         vmem((rank, 128)),
         dma((5,)),
-        dma((ROUNDS, 5)),
-        dma((ROUNDS, 5)),
-        dma((3,)),
-        dma((3,)),
-        dma((4, 2)),
-        dma((4, 2)),
-        dma((5, n_space)),
-        dma((5, n_space)),
-        dma((n_space,)),
-        dma((n_space,)),
+        dma((1,)),
+        dma((1,)),
+        dma((ROUNDS,)),
+        dma((5,)),
+        dma((5,)),
+        dma((1,)),
     ]
-    return pl.pallas_call(
+    done = pl.pallas_call(
         functools.partial(kernel, n_tm, n_space, rank),
         out_shape=(
-            jax.ShapeDtypeStruct((4, *state), F32),
-            jax.ShapeDtypeStruct((1, rank), F32),
+            pltpu.VMEM((4, *state), F32),
+            pltpu.VMEM((1, rank), F32),
         ),
         in_specs=[pl.BlockSpec(memory_space=pl.ANY)] * 4,
         out_specs=(
@@ -665,6 +667,16 @@
         scratch_shapes=scratch,
         compiler_params=pltpu.CompilerParams(collective_id=0, has_side_effects=True),
     )(speed, forcing, guess, basis)
+    return pl.pallas_call(
+        finish,
+        out_shape=(
+            jax.ShapeDtypeStruct((4, *state), F32),
+            jax.ShapeDtypeStruct((1, rank), F32),
+        ),
+        in_specs=[pl.BlockSpec(memory_space=pltpu.VMEM)] * 2,
+        out_specs=[pl.BlockSpec(memory_space=pl.ANY)] * 2,
+        scratch_shapes=[dma((2,))],
+    )(*(pltpu.with_memory_space_constraint(v, pltpu.VMEM) for v in done))
 
 
 def solution(mesh):

time: 95.9 us -> 83.4 us (0.87)
  Pallas kernels: 91.5 us -> 82.3 us
  local copies, waits for them, and re-layouts: 2.8 us -> 0 us
    pallas_call x1, Pallas kernels: 91.5 us -> 81.6 us  [body(): pl.pallas_call(functools.partial(kernel, n_tm, n_space, rank), out_shape=...]
    unnamed x2 -> x0, local copies, waits for them, and re-layouts: 2.8 us -> none
where the time goes in v2:
time: 83.4 us; the launch traced here: 83 us
  Pallas kernels  82.3 us (99%)
    pallas_call x1, Pallas kernels, body(): pl.pallas_call(functools.partial(kernel, n_tm, n_space, rank), out_shape=...  81.6 us

profile of v2, /device:TPU:0, one launch (start us, length us, event | category | flops | bytes accessed | tf_op | source)
XLA Modules:
  0.0 83.0 jit_solution(10518481178388807235)
XLA Ops:
  0.6 81.6 %shard_map.59 = (f32[4,4,2,16,128]{4,3,2,1,0:T(8,128)S(1)}, f32[1,64]{1,0:T(1,128)S(1)}) custom-call(f32[2,16,128]{2,1,0:T(8,128)} %speed_hbm.1, f32[4,2,16,128]{3,2,1,0:T(8,128)} %forcing_hbm.1, f32[1,4,2,16,128]{4,3,2,1,0:T(8,128)} %guess_hbm.1, f32[1,64,4,2,16,128]{5,4,3,2,1,0:T(8,128)} %basis_hbm.1), custom_call_target="tpu_custom_call" | custom-call | tf_op jit(solution)/shard_map/pallas_call | solution.py:656
  82.2 0.7 shard_map.60

commit v3 on v2

--- a/solution.py
+++ b/solution.py
@@ -52,6 +52,7 @@
     x_ref,
     gap_ref,
     fin_ref,
+    dual_ref,
     ar_ref,
     gram_ref,
     inv_ref,
@@ -287,24 +288,32 @@
         spread = jnp.where(diagonal, jnp.broadcast_to(column, (rank, 128)), 0.0)
         return jnp.sum(spread, axis=0, keepdims=True)
 
-    def share_products(i, state_ref):
-        def group(g, carry):
+    def products(name, columns, field, planes, more=False):
+        with jax.named_scope(name):
             out = []
-            for k in range(16):
-                total = jnp.zeros((8, 128), F32)
-                for c in range(4):
-                    for z in range(2):
-                        for half in range(nx // 8):
-                            part = slice(half * 8, half * 8 + 8)
-                            total = total + (
-                                b_ref[g * 16 + k, c, z, part, :] * state_ref[c, z, part, :]
-                            )
+            for r in range(rank):
+                total = None
+                for at in planes:
+                    for half in range(nx // 8):
+                        part = (*at, slice(half * 8, half * 8 + 8), slice(None))
+                        term = columns[(r, *part)] * field[part]
+                        total = term if total is None else total + term
                 out.append(jnp.sum(total, axis=0, keepdims=True))
-            part_ref[pl.ds(pl.multiple_of(g * 16, 16), 16), :] = jnp.concatenate(out, axis=0)
-            return carry
-
-        with jax.named_scope(f"products{i}"):
-            lax.fori_loop(0, rank // 16, group, 0)
+                if r % 8 == 7:
+                    block = jnp.concatenate(out, axis=0)
+                    if more:
+                        block = block + part_ref[r - 7 : r + 1, :]
+                    part_ref[r - 7 : r + 1, :] = block
+                    out = []
+
+    def full_products(name, field, more=False):
+        products(name, b_ref, field, [(c, z) for c in range(4) for z in range(2)], more)
+
+    def dual_products(name):
+        products(name, bm_ref, dual_ref, [(m,) for m in range(5)], True)
+
+    def share_products(i):
+        with jax.named_scope(f"share{i}"):
             ar_ref[i, s] = to_row(jnp.sum(part_ref[...], axis=1, keepdims=True))
             for j in far_first:
                 send(ar_ref.at[i, s], ar_ref.at[i, s], ar_sem.at[i], 0, j, ar_send_sem.at[i])
@@ -316,37 +325,47 @@
         total = ar_ref[i, 0]
         for j in range(1, n_space):
             total = total + ar_ref[i, j]
-        moved = pltpu.roll(jnp.broadcast_to(total, (8, 128)), rank, 1)[0:1]
-        product = jnp.where(lanes >= rank, inv_ref[...] * moved, 0.0)
-        return jnp.sum(product, axis=1, keepdims=True)
+        return jnp.sum(inv_ref[...] * total, axis=1, keepdims=True)
 
     def combine_columns(i, weights):
         w_ref[...] = jnp.broadcast_to(weights, (rank, 128))
 
         def group(g, acc):
-            for k in range(4):
-                r = g * 4 + k
+            for k in range(16):
+                r = g * 16 + k
                 w = jnp.broadcast_to(w_ref[pl.ds(r, 1), :], plane)
                 acc = tuple(acc[m] + w * bm_ref[r, m] for m in range(5))
             return acc
 
         with jax.named_scope(f"columns{i}"):
-            acc = lax.fori_loop(0, rank // 4, group, (zero,) * 5)
+            acc = lax.fori_loop(0, rank // 16, group, (zero,) * 5)
             for m in range(5):
                 msg_ref[i, m] = acc[m]
 
     def eliminate(low, high):
-        def step(k, carry):
+        def step(i, carry):
+            k = 2 * i
+            at0, at1 = lanes == 128 - rank + k, lanes == 128 - rank + k + 1
+
+            def pick(mask, v):
+                return jnp.sum(jnp.where(mask, v, 0.0), axis=1, keepdims=True)
+
             m = inv_ref[...]
-            row = inv_ref[pl.ds(k, 1), :]
-            col = jnp.sum(jnp.where(lanes == k, m, 0.0), axis=1, keepdims=True)
-            pivot = jnp.sum(jnp.where(lanes[0:1] == k, row, 0.0), axis=1, keepdims=True)
-            row = row / pivot
-            inv_ref[...] = jnp.where(rows == k, row, m - col * row)
+            row0, row1 = inv_ref[pl.ds(k, 1), :], inv_ref[pl.ds(k + 1, 1), :]
+            col0, col1 = pick(at0, m), pick(at1, m)
+            a, b = pick(at0[0:1], row0), pick(at1[0:1], row0)
+            c, d = pick(at0[0:1], row1), pick(at1[0:1], row1)
+            ratio = b / a
+            row0 = row0 / a
+            row1 = (row1 - c * row0) / (d - c * ratio)
+            row0 = row0 - ratio * row1
+            m = (m - col0 * row0) - col1 * row1
+            m = jnp.where(rows == k, row0, m)
+            inv_ref[...] = jnp.where(rows == k + 1, row1, m)
             return carry
 
         with jax.named_scope(f"eliminate{low}"):
-            lax.fori_loop(low, high, step, 0)
+            lax.fori_loop(low // 2, high // 2, step, 0)
 
     def wait_rows():
         with jax.named_scope("wait_bt"):
@@ -369,26 +388,38 @@
             preferred_element_type=F32,
         )
 
+    each = rank // n_space
+
     def send_gram():
         with jax.named_scope("gram"):
             acc = lax.fori_loop(0, 16, gram_part, jnp.zeros((3 * rank, 3 * rank), F32))
         acc = acc[2 * rank :] + acc[rank : 2 * rank] + acc[:rank]
         gram = acc[:, 2 * rank :] + acc[:, rank : 2 * rank] + acc[:, :rank]
-        half = rank // 2
-        gram_ref[s] = jnp.concatenate([gram[:half], gram[half:]], axis=1)
+        gram = jnp.concatenate([jnp.zeros((rank, 128 - rank), F32), gram], axis=1)
+        for o in range(n_space):
+            gram_ref[0, o] = gram[o * each : o * each + each]
+        gram_ref[1, s] = gram_ref[0, s]
         for j in far_first:
-            send(gram_ref.at[s], gram_ref.at[s], gram_sem.at[0], 0, j)
-
-    with jax.named_scope("wait_basis"):
-        loads[3].wait()
-
-    def column_msg(g, carry):
-        for k in range(8):
-            write_msg(bm_ref.at[g * 8 + k], load_state(b_ref.at[g * 8 + k]))
-        return carry
-
-    with jax.named_scope("column_msg"):
-        lax.fori_loop(0, rank // 8, column_msg, 0)
+            send(
+                gram_ref.at[0, at_s(j)], gram_ref.at[1, s], gram_sem.at[0], 0, j, gram_sem.at[2]
+            )
+
+    def wait_gram(k):
+        with jax.named_scope(f"wait_gram{k}"):
+            part = gram_ref.at[1, pl.ds(0, n_space - 1)]
+            pltpu.make_async_copy(part, part, gram_sem.at[k]).wait()
+
+    def share_gram():
+        wait_gram(0)
+        rows_sum = gram_ref[1, 0]
+        for o in range(1, n_space):
+            rows_sum = rows_sum + gram_ref[1, o]
+        gram_ref[2, s] = rows_sum
+        for j in far_first:
+            send(
+                gram_ref.at[2, s], gram_ref.at[2, s], gram_sem.at[1], 0, j, gram_sem.at[3]
+            )
+
     with jax.named_scope("barrier"):
         pl.semaphore_wait(barrier, len(peers))
 
@@ -405,7 +436,8 @@
         if edge[k] is None:
             pair = [
                 (speed_ref, speed_halo.at[k]),
-                (force_ref.at[pl.ds(0, 3)], force_halo.at[k]),
+                (force_ref.at[pl.ds(0, 2)], force_halo.at[k, pl.ds(0, 2)]),
+                (force_ref.at[2, pl.ds(1 - k, 1)], force_halo.at[k, 2, pl.ds(1 - k, 1)]),
             ]
         else:
             pair = [
@@ -421,7 +453,7 @@
     wait_rows()
     send_gram()
 
-    wait_round(R1, DEEP, 8 + 6 + 14)
+    wait_round(R1, DEEP, 8 + 6 + 12)
     for j, value, on in (
         (0, speed_ref[0], None),
         (1, speed_ref[1], None),
@@ -456,25 +488,23 @@
     send_halo(R2, DEEP, 1)
     send_state(R2, rel_ref, 1)
 
+    with jax.named_scope("wait_basis"):
+        loads[3].wait()
+
+    def column_msg(g, carry):
+        for k in range(8):
+            write_msg(bm_ref.at[g * 8 + k], load_state(b_ref.at[g * 8 + k]))
+        return carry
+
+    with jax.named_scope("column_msg"):
+        lax.fori_loop(0, rank // 8, column_msg, 0)
+    share_gram()
     wait_round(R2, DEEP, 8)
     residue = combine(lambda a, b: a - b, four_forced(R2), load_state(rel_ref))
     store_state(res_ref, residue)
     write_msg(msg_ref.at[R3], residue, deep=False)
-    send_state(R3, res_ref, 1)
+    send(res_ref, own_ref.at[R3], recv_sem.at[ROUNDS], 1, 0)
     send_halo(R3, ONE, 1)
-
-    with jax.named_scope("wait_gram"):
-        part = gram_ref.at[pl.ds(0, n_space - 1)]
-        pltpu.make_async_copy(part, part, gram_sem.at[0]).wait()
-    whole = gram_ref[0]
-    for j in range(1, n_space):
-        whole = whole + gram_ref[j]
-    half = rank // 2
-    unit = (lanes == rows + rank).astype(F32)
-    left = lanes[:half] < rank
-    inv_ref[0:half, :] = jnp.where(left, whole, unit[:half])
-    inv_ref[half:rank, :] = jnp.where(left, pltpu.roll(whole, 128 - rank, 1), unit[half:])
-    eliminate(0, 24)
 
 
     def coarse(state, halo):
@@ -489,63 +519,84 @@
     def correction(halo, own):
         p, d = unpack(halo, (own[1], own[2]), (own[0], own[4]), own[3], 4)
         values, first = steps(p, d, DT, 4)
-        out = [[None] * 2 for _ in range(4)]
+        moved = []
         for z in range(2):
             slow = p[z] - (4 * DT * c2(z)) * (d[z] - (4 * DT) * first[z])
-            out[0][z] = values[4][z] - slow
+            moved.append(values[4][z] - slow)
         total = {
             j: (values[1][j] - p[j]) + (values[2][j] - p[j]) + (values[3][j] - p[j])
             for j in range(0, 3)
         }
+        dual = (DT * total[0], moved[0], moved[1], -DT * total[2], DT * total[1])
+        for m in range(5):
+            dual_ref[m] = dual[m]
+        return moved, total
+
+    def corrected(state, moved, total):
+        out = [[state[0][z] + moved[z] for z in range(2)], [None] * 2, [None] * 2, [None] * 2]
         for z in range(2):
             for c, slope in enumerate(grad(total, z)):
-                out[c + 1][z] = -DT * slope
+                out[c + 1][z] = state[c + 1][z] - DT * slope
         return out
 
     def add(a, b):
         return a + b
 
-    def candidate(n, i_y, i_x, x_state_ref, last):
-        share_products(n, x_state_ref)
-        if i_x != R3:
-            wait_round(i_x, ONE, 0)
+    def candidate(n, i_y, i_x, x_state_ref):
+        last = i_y == Y4
+        if n == 0:
+            invert_gram()
+        wait_round(i_x, ONE, 0)
         z = combine(add, coarse(load_state(x_state_ref), halo_of(i_x)), load_state(res_ref))
-        store_state(zout_ref.at[n], z)
-        if not last:
-            send(zout_ref.at[n], zin_ref.at[n], recv_sem.at[i_y], 1, 0)
-        if n == 0:
-            eliminate(24, rank)
+        if last:
+            store_state(fin_ref, combine(add, z, load_state(rel_ref)))
+        else:
+            store_state(zout_ref.at[n], z)
+            send(zout_ref.at[n], zin_ref.at[n], recv_sem.at[ROUNDS + 1 + n], 1, 0)
         combine_columns(i_y, solved(n))
-        dt = 0 if last else 1
-        send_halo(i_y, DEEP, dt)
+        send_halo(i_y, DEEP, 0 if last else 1)
         if last:
+            full_products("products_last", fin_ref)
             wait_round(i_y, DEEP, 0)
-            return combine(
-                add,
-                load_state(zout_ref.at[n]),
-                correction(halo_of(i_y), msg_ref.at[i_y]),
-            )
-        send_own(i_y, msg_ref.at[i_y], yown_ref.at[n], dt)
-        wait_round(i_y, DEEP, 5 + 8)
-        return combine(
-            add, load_state(zin_ref.at[n]), correction(halo_of(i_y), yown_ref.at[n])
-        )
-
-    def announce(i, ref, state):
-        store_state(ref, state)
-        write_msg(msg_ref.at[i], state, deep=False)
+            return correction(halo_of(i_y), msg_ref.at[i_y])
+        send_own(i_y, msg_ref.at[i_y], yown_ref.at[n], 1)
+        with jax.named_scope(f"wait_z{n}"):
+            wait_planes(recv_sem.at[ROUNDS + 1 + n], 8)
+        full_products(f"products_z{n}", zin_ref.at[n])
+        wait_round(i_y, DEEP, 5)
+        return correction(halo_of(i_y), yown_ref.at[n])
+
+    def invert_gram():
+        wait_gram(1)
+        for o in range(n_space):
+            inv_ref[o * each : o * each + each, :] = gram_ref[2, o]
+        inv_ref[...] = inv_ref[...] + diagonal.astype(F32)
+        eliminate(0, rank)
+
+    def announce(i, state_ref, moved, total):
+        msg_ref[i, 1] = state_ref[0, 0] + moved[0]
+        msg_ref[i, 2] = state_ref[0, 1] + moved[1]
+        msg_ref[i, 3] = state_ref[3, 1] - DT * (total[2] - total[1])
         send_halo(i, ONE, 0)
 
-    wait_round(R3, ONE, 8)
-    announce(X2, x_ref.at[0], candidate(0, Y1, R3, own_ref.at[R3], False))
-    announce(X3, x_ref.at[1], candidate(1, Y2, X2, x_ref.at[0], False))
-    third = candidate(2, Y3, X3, x_ref.at[1], False)
-    store_state(x_ref.at[2], third)
+    with jax.named_scope("wait_res"):
+        wait_planes(recv_sem.at[ROUNDS], 8)
+    full_products("products0", own_ref.at[R3])
+    share_products(0)
+    for n, (i_y, i_x, ref) in enumerate(
+        ((Y1, R3, own_ref.at[R3]), (Y2, X2, x_ref.at[0]))
+    ):
+        moved, total = candidate(n, i_y, i_x, ref)
+        announce(X2 + n, zin_ref.at[n], moved, total)
+        dual_products(f"products{n + 1}")
+        share_products(n + 1)
+        store_state(x_ref.at[n], corrected(load_state(zin_ref.at[n]), moved, total))
+    moved, total = candidate(2, Y3, X3, x_ref.at[1])
+    third = corrected(load_state(zin_ref.at[2]), moved, total)
 
     gap = combine(lambda a, b: a - b, third, load_state(x_ref.at[1]))
     store_state(gap_ref, gap)
     write_msg(msg_ref.at[GAP], gap)
-    store_state(x_ref.at[3], third)
     early = jnp.logical_and(t >= 1, t <= n_tm - 4)
     late = jnp.logical_or(t == 0, t >= n_tm - 3)
 
@@ -553,6 +604,9 @@
     def _():
         send_halo(GAP, TWO, 4, gap_sem.at[0])
         send_state(GAP, gap_ref, 4, gap_sem.at[0])
+
+    store_state(x_ref.at[2], third)
+    dual_products("products3")
 
     @pl.when(late)
     def _():
@@ -565,18 +619,26 @@
         for z in range(2):
             for c, slope in enumerate(grad(total, z)):
                 behind[c + 1][z] = state[c + 1][z] - (8 * DT) * slope
-        store_state(x_ref.at[3], combine(add, load_state(x_ref.at[2]), behind))
-
-    write_msg(msg_ref.at[X4], load_state(x_ref.at[3]), deep=False)
+        store_state(x_ref.at[3], behind)
+        store_state(x_ref.at[2], combine(add, load_state(x_ref.at[2]), behind))
+
+    write_msg(msg_ref.at[X4], load_state(x_ref.at[2]), deep=False)
     send_halo(X4, ONE, 0)
-    levels = candidate(3, Y4, X4, x_ref.at[3], True)
-
-    final = combine(add, load_state(rel_ref), levels)
+
+    @pl.when(late)
+    def _():
+        full_products("products_gap", x_ref.at[3], True)
+
+    share_products(3)
+    moved, total = candidate(3, Y4, X4, x_ref.at[2])
+
+    final = corrected(load_state(fin_ref), moved, total)
     store_state(fin_ref, final)
     write_msg(msg_ref.at[LAST], final)
     send_halo(LAST, THREE, 1)
     send_state(LAST, fin_ref, 1)
-    share_products(4, fin_ref)
+    dual_products("products4")
+    share_products(4)
     store_state(states_ref.at[3], final)
     wait_round(LAST, THREE, 8)
     state = load_state(own_ref.at[LAST])
@@ -591,7 +653,11 @@
     coords_ref[...] = to_row(solved(4))[:, :rank]
 
     with jax.named_scope("wait_sends"):
-        wait_planes(send_sem.at[0], sum(sent) // math.prod(plane))
+        planes, odd = divmod(sum(sent), math.prod(plane))
+        assert odd == 0
+        wait_planes(send_sem.at[0], planes)
+        for k in (2, 3):
+            wait_gram(k)
         for i in range(5):
             part = ar_ref.at[i, pl.ds(0, n_space - 1)]
             pltpu.make_async_copy(part, part, ar_send_sem.at[i]).wait()
@@ -640,18 +706,19 @@
         vmem((4, *state)),
         vmem(state),
         vmem(state),
+        vmem(msg),
         vmem((5, n_space, 1, 128)),
-        vmem((n_space, rank // 2, 128)),
+        vmem((3, n_space, rank // n_space, 128)),
         vmem((rank, 128)),
         vmem((rank, 128)),
         vmem((rank, 128)),
         dma((5,)),
         dma((1,)),
         dma((1,)),
-        dma((ROUNDS,)),
+        dma((ROUNDS + 4,)),
         dma((5,)),
         dma((5,)),
-        dma((1,)),
+        dma((4,)),
     ]
     done = pl.pallas_call(
         functools.partial(kernel, n_tm, n_space, rank),

time: 83.4 us -> 79.5 us (0.953)
  Pallas kernels: 82.3 us -> 78.2 us
    pallas_call x1, Pallas kernels: 81.6 us -> 77.5 us  [body(): pl.pallas_call(functools.partial(kernel, n_tm, n_space, rank), out_shape=...]
where the time goes in v3:
time: 79.5 us; the launch traced here: 78.8 us
  Pallas kernels  78.2 us (98%)
    pallas_call x1, Pallas kernels, body(): pl.pallas_call(functools.partial(kernel, n_tm, n_space, rank), out_shape=...  77.5 us

profile of v3, /device:TPU:0, one launch (start us, length us, event | category | flops | bytes accessed | tf_op | source)
XLA Modules:
  0.0 78.8 jit_solution(13304695387629137312)
XLA Ops:
  0.6 77.5 %shard_map.59 = (f32[4,4,2,16,128]{4,3,2,1,0:T(8,128)S(1)}, f32[1,64]{1,0:T(1,128)S(1)}) custom-call(f32[2,16,128]{2,1,0:T(8,128)} %speed_hbm.1, f32[4,2,16,128]{3,2,1,0:T(8,128)} %forcing_hbm.1, f32[1,4,2,16,128]{4,3,2,1,0:T(8,128)} %guess_hbm.1, f32[1,64,4,2,16,128]{5,4,3,2,1,0:T(8,128)} %basis_hbm.1), custom_call_target="tpu_custom_call" | custom-call | tf_op jit(solution)/shard_map/pallas_call | solution.py:723
  78.1 0.7 shard_map.60

commit v4 on v3

--- a/solution.py
+++ b/solution.py
@@ -76,6 +76,24 @@
     def at_s(d):
         return lax.rem(s + (d + n_space), n_space)
 
+    inner = jnp.logical_and(s >= 2, s <= n_space - 3)
+    edge = jnp.logical_not(inner)
+    has = {0: None, 1: s <= n_space - 2, -1: s >= 1, 2: s <= n_space - 3, -2: s >= 2}
+    edges = ((0, (-1, -2)), (1, (-2,)), (n_space - 2, (2,)), (n_space - 1, (1, 2)))
+
+    def where_it_is(act):
+        @pl.when(inner)
+        def _():
+            act(())
+
+        @pl.when(edge)
+        def _():
+            for place, out in edges:
+
+                @pl.when(s == place)
+                def _(out=out):
+                    act(out)
+
     loads = [
         pltpu.make_async_copy(guess_hbm.at[0], guess_ref, local_sem.at[0]),
         pltpu.make_async_copy(speed_hbm, speed_ref, local_sem.at[1]),
@@ -85,6 +103,8 @@
     for load in loads:
         load.start()
 
+    far_first = sorted(range(1, n_space), key=lambda j: abs(abs(j - n_space // 2) - 2))
+
     def start_rows(m, carry):
         c = m // 2
         z = lax.rem(m, 2)
@@ -94,24 +114,56 @@
             ).start()
         return carry
 
+    @pl.when(edge)
+    def _():
+        def clear(i, carry):
+            for k in range(4):
+                for m in range(5):
+                    halo_ref[i, k, m] = jnp.zeros(plane, F32)
+            return carry
+
+        lax.fori_loop(0, ROUNDS, clear, 0)
+        for k in range(4):
+            for z in range(2):
+                speed_halo[k, z] = jnp.zeros(plane, F32)
+                for n in range(3):
+                    force_halo[k, n, z] = jnp.zeros(plane, F32)
+
     barrier = pltpu.get_barrier_semaphore()
-    peers = [(dt, ds) for dt in (1, -1) for ds in (-2, -1, 0, 1, 2)]
-    peers += [(4, ds) for ds in (-1, 0, 1)]
-    peers += [(0, ds) for ds in range(1, n_space)]
+    count = 0
     with jax.named_scope("signals"):
-        for dt, ds in peers:
+
+        def greet(dt, ds):
             pl.semaphore_signal(
                 barrier, inc=1, device_id=(at_t(dt), at_s(ds)), device_id_type=MESH
             )
+
+        for ds in (2, -2, 1, -1, 0):
+            near = (1, -1, 4) if abs(ds) < 2 else (1, -1)
+            if has[ds] is None:
+                count = count + len(near)
+                for dt in near:
+                    greet(dt, ds)
+            else:
+                count = count + len(near) * has[ds].astype(jnp.int32)
+
+                @pl.when(has[ds])
+                def _(near=near, ds=ds):
+                    for dt in near:
+                        greet(dt, ds)
+
+        for ds in far_first:
+            count = count + 1
+            greet(0, ds)
     with jax.named_scope("rows"):
         lax.fori_loop(0, 8, start_rows, 0)
 
-    sent = []
+    sent = {offset: 0 for offset in has}
 
     def words(ref):
         return math.prod(ref.shape)
 
-    def send(src, dst, rsem, dt, ds, ssem=None):
+    def send(src, dst, rsem, dt, ds, ssem=None, tally=True):
         pltpu.make_async_remote_copy(
             src_ref=src,
             dst_ref=dst,
@@ -120,8 +172,8 @@
             device_id=(at_t(dt), at_s(ds)),
             device_id_type=MESH,
         ).start()
-        if ssem is None:
-            sent.append(words(src))
+        if ssem is None and tally:
+            sent[ds] += words(src)
 
     def wait_planes(sem, planes):
         part = bm_ref.reshape(rank * 5, *plane).at[pl.ds(0, planes)]
@@ -250,20 +302,27 @@
         return p, d
 
     def send_halo(i, slices, dt, ssem=None):
-        for k in reversed(range(len(slices))):
-            low, high = slices[k]
-            part = pl.ds(low, high - low)
-            send(
-                msg_ref.at[i, part],
-                halo_ref.at[i, k, part],
-                recv_sem.at[i],
-                dt,
-                OFFSETS[k],
-                ssem,
-            )
-
-    def planes_of(slices):
-        return sum(high - low for low, high in slices)
+        def act(out):
+            for k in reversed(range(len(slices))):
+                if OFFSETS[k] not in out:
+                    low, high = slices[k]
+                    part = pl.ds(low, high - low)
+                    send(
+                        msg_ref.at[i, part],
+                        halo_ref.at[i, k, part],
+                        recv_sem.at[i],
+                        dt,
+                        OFFSETS[k],
+                        ssem,
+                        out == (),
+                    )
+
+        where_it_is(act)
+
+    def planes_of(slices, out=()):
+        return sum(
+            high - low for k, (low, high) in enumerate(slices) if -OFFSETS[k] not in out
+        )
 
     def send_own(i, src, dst, dt, ssem=None):
         send(src, dst, recv_sem.at[i], dt, 0, ssem)
@@ -273,7 +332,9 @@
 
     def wait_round(i, slices, more):
         with jax.named_scope(f"wait_round{i}"):
-            wait_planes(recv_sem.at[i], planes_of(slices) + more)
+            where_it_is(
+                lambda out: wait_planes(recv_sem.at[i], planes_of(slices, out) + more)
+            )
 
     def halo_of(i):
         return halo_ref.at[i]
@@ -281,8 +342,6 @@
     rows = lax.broadcasted_iota(jnp.int32, (rank, 128), 0)
     lanes = lax.broadcasted_iota(jnp.int32, (rank, 128), 1)
     diagonal = rows == lanes
-
-    far_first = sorted(range(1, n_space), key=lambda j: abs(abs(j - n_space // 2) - 2))
 
     def to_row(column):
         spread = jnp.where(diagonal, jnp.broadcast_to(column, (rank, 128)), 0.0)
@@ -421,7 +480,7 @@
             )
 
     with jax.named_scope("barrier"):
-        pl.semaphore_wait(barrier, len(peers))
+        pl.semaphore_wait(barrier, count)
 
     with jax.named_scope("wait_guess"):
         loads[0].wait()
@@ -431,29 +490,34 @@
     with jax.named_scope("wait_load12"):
         loads[1].wait()
         loads[2].wait()
-    edge = (None, None, pl.ds(1, 1), pl.ds(0, 1))
-    for k in (3, 2, 1, 0):
-        if edge[k] is None:
-            pair = [
-                (speed_ref, speed_halo.at[k]),
-                (force_ref.at[pl.ds(0, 2)], force_halo.at[k, pl.ds(0, 2)]),
-                (force_ref.at[2, pl.ds(1 - k, 1)], force_halo.at[k, 2, pl.ds(1 - k, 1)]),
-            ]
-        else:
-            pair = [
-                (speed_ref.at[edge[k]], speed_halo.at[k, edge[k]]),
-                (
-                    force_ref.at[pl.ds(0, 1), edge[k]],
-                    force_halo.at[k, pl.ds(0, 1), edge[k]],
-                ),
-            ]
-        for src, dst in pair:
-            send(src, dst, recv_sem.at[R1], 0, OFFSETS[k])
+    around = (
+        ((slice(0, 2), slice(0, 2)), (slice(2, 3), slice(1, 2))),
+        ((slice(0, 2), slice(0, 2)), (slice(2, 3), slice(0, 1))),
+        ((slice(0, 1), slice(1, 2)),),
+        ((slice(0, 1), slice(0, 1)),),
+    )
+
+    def part_of(cut):
+        return pl.ds(cut.start, cut.stop - cut.start)
+
+    def send_start(out):
+        for k in (3, 2, 1, 0):
+            if OFFSETS[k] in out:
+                continue
+            planes = part_of(around[k][0][1])
+            pairs = [(speed_ref.at[planes], speed_halo.at[k, planes])]
+            for steps_cut, planes_cut in around[k]:
+                at = (part_of(steps_cut), part_of(planes_cut))
+                pairs.append((force_ref.at[at], force_halo.at[(k, *at)]))
+            for src, dst in pairs:
+                send(src, dst, recv_sem.at[R1], 0, OFFSETS[k], None, out == ())
+
+    where_it_is(send_start)
 
     wait_rows()
     send_gram()
 
-    wait_round(R1, DEEP, 8 + 6 + 12)
+    wait_round(R1, tuple((low, high + n) for (low, high), n in zip(DEEP, (7, 7, 2, 2))), 8)
     for j, value, on in (
         (0, speed_ref[0], None),
         (1, speed_ref[1], None),
@@ -653,9 +717,13 @@
     coords_ref[...] = to_row(solved(4))[:, :rank]
 
     with jax.named_scope("wait_sends"):
-        planes, odd = divmod(sum(sent), math.prod(plane))
-        assert odd == 0
-        wait_planes(send_sem.at[0], planes)
+        def wait_sent(out):
+            total = sum(n for offset, n in sent.items() if offset not in out)
+            planes, odd = divmod(total, math.prod(plane))
+            assert odd == 0
+            wait_planes(send_sem.at[0], planes)
+
+        where_it_is(wait_sent)
         for k in (2, 3):
             wait_gram(k)
         for i in range(5):
@@ -664,7 +732,10 @@
 
         @pl.when(early)
         def _():
-            wait_planes(gap_sem.at[0], planes_of(TWO) + 8)
+            def wait_gap(out):
+                wait_planes(gap_sem.at[0], 8 + 4 * (1 not in out) + 3 * (-1 not in out))
+
+            where_it_is(wait_gap)
 
 
 def finish(states_ref, coords_ref, states_out, coords_out, sem):

time: 79.5 us -> 74 us (0.931)
  Pallas kernels: 78.2 us -> 73.2 us
    pallas_call x1, Pallas kernels: 77.5 us -> 72.5 us  [body(): pl.pallas_call(functools.partial(kernel, n_tm, n_space, rank), out_shape=...]
where the time goes in v4:
time: 74 us; the launch traced here: 73.9 us
  Pallas kernels  73.2 us (99%)
    pallas_call x1, Pallas kernels, body(): pl.pallas_call(functools.partial(kernel, n_tm, n_space, rank), out_shape=...  72.5 us

profile of v4, /device:TPU:0, one launch (start us, length us, event | category | flops | bytes accessed | tf_op | source)
XLA Modules:
  0.0 73.9 jit_solution(16988356962313437793)
XLA Ops:
  0.6 72.5 %shard_map.59 = (f32[4,4,2,16,128]{4,3,2,1,0:T(8,128)S(1)}, f32[1,64]{1,0:T(1,128)S(1)}) custom-call(f32[2,16,128]{2,1,0:T(8,128)} %speed_hbm.1, f32[4,2,16,128]{3,2,1,0:T(8,128)} %forcing_hbm.1, f32[1,4,2,16,128]{4,3,2,1,0:T(8,128)} %guess_hbm.1, f32[1,64,4,2,16,128]{5,4,3,2,1,0:T(8,128)} %basis_hbm.1), custom_call_target="tpu_custom_call" | custom-call | tf_op jit(solution)/shard_map/pallas_call | solution.py:794
  73.1 0.7 shard_map.60

commit v5 on v4

--- a/solution.py
+++ b/solution.py
@@ -17,7 +17,7 @@
 
 DEEP = ((0, 5), (0, 5), (1, 5), (0, 3))
 THREE = ((0, 5), (0, 5), (2, 4), (1, 2))
-TWO = ((1, 5), (0, 3))
+TWO = ((2, 5), (0, 2))
 ONE = ((2, 4), (1, 2))
 OFFSETS = (1, -1, 2, -2)
 
@@ -114,21 +114,6 @@
             ).start()
         return carry
 
-    @pl.when(edge)
-    def _():
-        def clear(i, carry):
-            for k in range(4):
-                for m in range(5):
-                    halo_ref[i, k, m] = jnp.zeros(plane, F32)
-            return carry
-
-        lax.fori_loop(0, ROUNDS, clear, 0)
-        for k in range(4):
-            for z in range(2):
-                speed_halo[k, z] = jnp.zeros(plane, F32)
-                for n in range(3):
-                    force_halo[k, n, z] = jnp.zeros(plane, F32)
-
     barrier = pltpu.get_barrier_semaphore()
     count = 0
     with jax.named_scope("signals"):
@@ -441,7 +426,7 @@
         low = (rest - middle.astype(F32)).astype(jnp.bfloat16)
         stacked = jnp.concatenate([high, middle, low], axis=0)
         return acc + lax.dot_general(
-            stacked,
+            stacked[: 2 * rank],
             stacked,
             (((1,), (1,)), ((), ())),
             preferred_element_type=F32,
@@ -451,9 +436,10 @@
 
     def send_gram():
         with jax.named_scope("gram"):
-            acc = lax.fori_loop(0, 16, gram_part, jnp.zeros((3 * rank, 3 * rank), F32))
-        acc = acc[2 * rank :] + acc[rank : 2 * rank] + acc[:rank]
-        gram = acc[:, 2 * rank :] + acc[:, rank : 2 * rank] + acc[:, :rank]
+            acc = lax.fori_loop(0, 16, gram_part, jnp.zeros((2 * rank, 3 * rank), F32))
+        acc = acc[rank:] + acc[:rank]
+        corner = acc[:, 2 * rank :]
+        gram = (corner + corner.T) + acc[:, rank : 2 * rank] + acc[:, :rank]
         gram = jnp.concatenate([jnp.zeros((rank, 128 - rank), F32), gram], axis=1)
         for o in range(n_space):
             gram_ref[0, o] = gram[o * each : o * each + each]
@@ -485,8 +471,6 @@
     with jax.named_scope("wait_guess"):
         loads[0].wait()
     write_msg(msg_ref.at[R1], load_state(guess_ref))
-    send_halo(R1, DEEP, 1)
-    send_state(R1, guess_ref, 1)
     with jax.named_scope("wait_load12"):
         loads[1].wait()
         loads[2].wait()
@@ -504,6 +488,16 @@
         for k in (3, 2, 1, 0):
             if OFFSETS[k] in out:
                 continue
+            part = part_of(slice(*DEEP[k]))
+            send(
+                msg_ref.at[R1, part],
+                halo_ref.at[R1, k, part],
+                recv_sem.at[R1],
+                1,
+                OFFSETS[k],
+                None,
+                out == (),
+            )
             planes = part_of(around[k][0][1])
             pairs = [(speed_ref.at[planes], speed_halo.at[k, planes])]
             for steps_cut, planes_cut in around[k]:
@@ -513,6 +507,24 @@
                 send(src, dst, recv_sem.at[R1], 0, OFFSETS[k], None, out == ())
 
     where_it_is(send_start)
+    send_state(R1, guess_ref, 1)
+
+    def clear(out):
+        for k in range(4):
+            if -OFFSETS[k] in out:
+
+                def clear_round(i, carry, k=k):
+                    for m in range(5):
+                        halo_ref[i, k, m] = zero
+                    return carry
+
+                lax.fori_loop(0, ROUNDS, clear_round, 0)
+                for z in range(2):
+                    speed_halo[k, z] = zero
+                    for n in range(3):
+                        force_halo[k, n, z] = zero
+
+    where_it_is(clear)
 
     wait_rows()
     send_gram()
@@ -602,6 +614,41 @@
             for c, slope in enumerate(grad(total, z)):
                 out[c + 1][z] = state[c + 1][z] - DT * slope
         return out
+
+    def write_edges(ref, state):
+        h, p = 8 * DT, state[0]
+        low, high = divergence(state)
+        none = {-1: zero, 0: p[0], 1: p[1], 2: zero}
+
+        def inside(j):
+            return (
+                (x_ahead(p[j]) + x_behind(p[j]))
+                + (y_ahead(p[j]) + y_behind(p[j]))
+                + (none[j + 1] - weight * p[j])
+                + (none[j - 1] - p[j])
+            )
+
+        ref[0] = p[0] - (h * c2(0)) * (low - h * inside(0))
+        ref[4] = p[1] - (h * c2(1)) * (high - h * inside(1))
+        ref[1] = p[0]
+        ref[2] = p[1]
+        ref[3] = state[3][1]
+
+    def two_steps(state, halo):
+        h = 8 * DT
+        low, high = divergence(state)
+        p = {0: state[0][0], 1: state[0][1], -1: halo[0, 2] * e_dn1, 2: halo[1, 1] * e_up1}
+        d = {0: low - halo[0, 3] * e_dn1, 1: high}
+        values = [p]
+        for n in range(2):
+            d = {j: d[j] - h * lap(p, j) for j in range(2)}
+            after = {j: p[j] - (h * c2(j)) * d[j] for j in range(2)}
+            if n == 0:
+                after[-1] = halo[0, 4] * e_dn1 + (h * h * c2(-1)) * p[0]
+                after[2] = halo[1, 0] * e_up1 + (h * c2(2)) * (state[3][1] + h * p[1])
+            p = after
+            values.append(p)
+        return values
 
     def add(a, b):
         return a + b
@@ -651,16 +698,16 @@
         ((Y1, R3, own_ref.at[R3]), (Y2, X2, x_ref.at[0]))
     ):
         moved, total = candidate(n, i_y, i_x, ref)
-        announce(X2 + n, zin_ref.at[n], moved, total)
         dual_products(f"products{n + 1}")
         share_products(n + 1)
+        announce(X2 + n, zin_ref.at[n], moved, total)
         store_state(x_ref.at[n], corrected(load_state(zin_ref.at[n]), moved, total))
     moved, total = candidate(2, Y3, X3, x_ref.at[1])
     third = corrected(load_state(zin_ref.at[2]), moved, total)
 
     gap = combine(lambda a, b: a - b, third, load_state(x_ref.at[1]))
     store_state(gap_ref, gap)
-    write_msg(msg_ref.at[GAP], gap)
+    write_edges(msg_ref.at[GAP], gap)
     early = jnp.logical_and(t >= 1, t <= n_tm - 4)
     late = jnp.logical_or(t == 0, t >= n_tm - 3)
 
@@ -676,33 +723,29 @@
     def _():
         wait_round(GAP, TWO, 8)
         state = load_state(own_ref.at[GAP])
-        p, d = unpack(halo_of(GAP), state[0], divergence(state), state[3][1], 2)
-        values, _ = steps(p, d, 8 * DT, 2)
+        values = two_steps(state, halo_of(GAP))
         total = {j: values[0][j] + values[1][j] for j in range(0, 3)}
         behind = [[values[2][0], values[2][1]], [None] * 2, [None] * 2, [None] * 2]
         for z in range(2):
             for c, slope in enumerate(grad(total, z)):
                 behind[c + 1][z] = state[c + 1][z] - (8 * DT) * slope
         store_state(x_ref.at[3], behind)
+        full_products("products_gap", x_ref.at[3], True)
         store_state(x_ref.at[2], combine(add, load_state(x_ref.at[2]), behind))
 
+    share_products(3)
     write_msg(msg_ref.at[X4], load_state(x_ref.at[2]), deep=False)
     send_halo(X4, ONE, 0)
-
-    @pl.when(late)
-    def _():
-        full_products("products_gap", x_ref.at[3], True)
-
-    share_products(3)
     moved, total = candidate(3, Y4, X4, x_ref.at[2])
+
+    dual_products("products4")
+    share_products(4)
 
     final = corrected(load_state(fin_ref), moved, total)
     store_state(fin_ref, final)
     write_msg(msg_ref.at[LAST], final)
     send_halo(LAST, THREE, 1)
     send_state(LAST, fin_ref, 1)
-    dual_products("products4")
-    share_products(4)
     store_state(states_ref.at[3], final)
     wait_round(LAST, THREE, 8)
     state = load_state(own_ref.at[LAST])
@@ -733,7 +776,7 @@
         @pl.when(early)
         def _():
             def wait_gap(out):
-                wait_planes(gap_sem.at[0], 8 + 4 * (1 not in out) + 3 * (-1 not in out))
+                wait_planes(gap_sem.at[0], 8 + 3 * (1 not in out) + 2 * (-1 not in out))
 
             where_it_is(wait_gap)
 

time: 74 us -> 73.3 us (level)
  Pallas kernels: 73.2 us -> 72.2 us
    pallas_call x1, Pallas kernels: 72.5 us -> 71.5 us  [body(): pl.pallas_call(functools.partial(kernel, n_tm, n_space, rank), out_shape=...]
where the time goes in v5:
time: 73.3 us; the launch traced here: 72.8 us
  Pallas kernels  72.2 us (98%)
    pallas_call x1, Pallas kernels, body(): pl.pallas_call(functools.partial(kernel, n_tm, n_space, rank), out_shape=...  71.5 us

profile of v5, /device:TPU:0, one launch (start us, length us, event | category | flops | bytes accessed | tf_op | source)
XLA Modules:
  0.0 72.8 jit_solution(14042605736238672778)
XLA Ops:
  0.6 71.5 %shard_map.59 = (f32[4,4,2,16,128]{4,3,2,1,0:T(8,128)S(1)}, f32[1,64]{1,0:T(1,128)S(1)}) custom-call(f32[2,16,128]{2,1,0:T(8,128)} %speed_hbm.1, f32[4,2,16,128]{3,2,1,0:T(8,128)} %forcing_hbm.1, f32[1,4,2,16,128]{4,3,2,1,0:T(8,128)} %guess_hbm.1, f32[1,64,4,2,16,128]{5,4,3,2,1,0:T(8,128)} %basis_hbm.1), custom_call_target="tpu_custom_call" | custom-call | tf_op jit(solution)/shard_map/pallas_call | solution.py:837
  72.1 0.7 shard_map.60

commit v6 on v5

--- a/solution.py
+++ b/solution.py
@@ -375,14 +375,14 @@
         w_ref[...] = jnp.broadcast_to(weights, (rank, 128))
 
         def group(g, acc):
-            for k in range(16):
-                r = g * 16 + k
+            for k in range(32):
+                r = g * 32 + k
                 w = jnp.broadcast_to(w_ref[pl.ds(r, 1), :], plane)
                 acc = tuple(acc[m] + w * bm_ref[r, m] for m in range(5))
             return acc
 
         with jax.named_scope(f"columns{i}"):
-            acc = lax.fori_loop(0, rank // 16, group, (zero,) * 5)
+            acc = lax.fori_loop(0, rank // 32, group, (zero,) * 5)
             for m in range(5):
                 msg_ref[i, m] = acc[m]
 
@@ -698,9 +698,9 @@
         ((Y1, R3, own_ref.at[R3]), (Y2, X2, x_ref.at[0]))
     ):
         moved, total = candidate(n, i_y, i_x, ref)
+        announce(X2 + n, zin_ref.at[n], moved, total)
         dual_products(f"products{n + 1}")
         share_products(n + 1)
-        announce(X2 + n, zin_ref.at[n], moved, total)
         store_state(x_ref.at[n], corrected(load_state(zin_ref.at[n]), moved, total))
     moved, total = candidate(2, Y3, X3, x_ref.at[1])
     third = corrected(load_state(zin_ref.at[2]), moved, total)

time: 73.3 us -> 72.7 us (level)
  no operation moved by 1% of the time
where the time goes in v6:
time: 72.7 us; the launch traced here: 72.5 us
  Pallas kernels  71.9 us (99%)
    pallas_call x1, Pallas kernels, body(): pl.pallas_call(functools.partial(kernel, n_tm, n_space, rank), out_shape=...  71.2 us

profile of v6, /device:TPU:0, one launch (start us, length us, event | category | flops | bytes accessed | tf_op | source)
XLA Modules:
  0.0 72.5 jit_solution(3006554038223702918)
XLA Ops:
  0.6 71.2 %shard_map.59 = (f32[4,4,2,16,128]{4,3,2,1,0:T(8,128)S(1)}, f32[1,64]{1,0:T(1,128)S(1)}) custom-call(f32[2,16,128]{2,1,0:T(8,128)} %speed_hbm.1, f32[4,2,16,128]{3,2,1,0:T(8,128)} %forcing_hbm.1, f32[1,4,2,16,128]{4,3,2,1,0:T(8,128)} %guess_hbm.1, f32[1,64,4,2,16,128]{5,4,3,2,1,0:T(8,128)} %basis_hbm.1), custom_call_target="tpu_custom_call" | custom-call | tf_op jit(solution)/shard_map/pallas_call | solution.py:837
  71.8 0.7 shard_map.60
